TPU v7x, 256 devices: a whole 4x4x8 slice. The times are simulated.
256 devices in a mesh: slab: 128 (over x, z, y), pencil: 2 (over core).
Axes of the slice: x: 4, y: 4, z: 8, core: 2. Of those that a mesh axis runs over, the one named last changes fastest.
Arguments:
- density: float32 [768, 768, 384], P('slab', 'pencil'), may hold values from 0 to 1
- cell_kind: int32 [768, 768, 384], P('slab', 'pencil'), may hold values from 0 to 2
- sharpness: float32 [1], replicated, may hold values from 48 to 96
- fraction: float32 [1], replicated, may hold values from 0.36 to 0.41
Outputs:
- physical: float32 [768, 768, 384], P('slab', 'pencil')
- threshold: float32 [1], replicated
Inputs may be any that keep to these rules, and one draw needn't show every extreme that they name: `cell_kind`: each cell is a design, void or solid cell.
All inputs are finite; a program needn't handle non-finite values.
Results may differ from a plain program's by a relative error of at most 0.0003.
Values sent between devices are 32-bit elements; how exact they have to be, the bound alone decides.
No kernel may reach another device: no remote copies, remote signals or barrier semaphores. Data moves between devices by JAX's collectives and lax.ppermute only.
A program may use at most 128 MiB of HBM per device.

v0:
```python
import functools

import jax
import jax.numpy as jnp
from jax import lax
from jax.experimental import pallas as pl
from jax.experimental.pallas import tpu as pltpu


RADIUS = 5
ITERS = 3
REACH = 8
MOST = 112
FAR = 1e30
LIMIT = 16 << 20
CHUNKS = ((320, 384), (0, 128), (176, 320), (128, 176))
DEVICES = ("slab", "pencil")


VMEM = pl.BlockSpec(memory_space=pltpu.VMEM)
SMEM = pl.BlockSpec(memory_space=pltpu.SMEM)


def call(kernel, outs, ins, out_specs, in_specs, scratch=(), flops=0, moved=0):
    return pl.pallas_call(
        kernel,
        out_shape=outs,
        in_specs=in_specs,
        out_specs=out_specs,
        scratch_shapes=list(scratch),
        compiler_params=pltpu.CompilerParams(vmem_limit_bytes=LIMIT),
        cost_estimate=pl.CostEstimate(flops=flops, bytes_accessed=moved, transcendentals=0),
    )(*ins)


def along_z(layers, depth):
    pairs = [a + b for a, b in zip(layers[:-1], layers[1:])]
    sixes = [pairs[i] + pairs[i + 2] + pairs[i + 4] for i in range(depth + RADIUS)]
    pairs = [a + b for a, b in zip(sixes[:-1], sixes[1:])]
    return [pairs[i] + pairs[i + 2] + pairs[i + 4] for i in range(depth)]


def parts(x):
    high = x.astype(jnp.bfloat16)
    return high, (x - high.astype(jnp.float32)).astype(jnp.bfloat16)


def filter_zx(density, start, below, above, weights, out, high, low):
    depth, rows, cols = out.shape
    for r in range(0, rows, 16):
        for c in range(0, cols, 128):
            at = (slice(r, r + 16), slice(c, c + 128))
            layers = [below[(i, *at)] for i in range(RADIUS)]
            layers += [density[i, start + r : start + r + 16, c : c + 128] for i in range(depth)]
            layers += [above[(i, *at)] for i in range(RADIUS)]
            for i, value in enumerate(along_z(layers, depth)):
                high[(i, *at)], low[(i, *at)] = parts(value)
    w = weights[...]
    for i in range(depth):
        total = jnp.dot(low[i], w, preferred_element_type=jnp.float32)
        out[i] = total + jnp.dot(high[i], w, preferred_element_type=jnp.float32)


def zx_kernel(chunks, density, weights, _, *refs):
    halos, (out, tail, head, high, low) = refs[: 2 * len(chunks)], refs[2 * len(chunks) :]
    first = 0
    for n, (start, end) in enumerate(chunks):
        rows = pl.ds(first, end - start)
        first += end - start
        own = [r.at[:, rows, :] for r in (out, high, low)]
        filter_zx(density, start, *halos[2 * n : 2 * n + 2], weights, *own)
    edge, turn = chunks[0][1] - chunks[0][0], first - (chunks[-1][1] - chunks[-1][0])
    tail[...] = out[:, edge - REACH : edge, :]
    head[...] = out[:, turn : turn + REACH, :]


def zx(chunks, density, halos, weights, earlier):
    depth, cols = density.shape[0], density.shape[2]
    rows = sum(end - start for start, end in chunks)
    shape = lambda r: jax.ShapeDtypeStruct((depth, r, cols), jnp.float32)
    return call(
        functools.partial(zx_kernel, chunks),
        (shape(rows), shape(REACH), shape(REACH)),
        (density, weights, earlier, *(h for pair in halos for h in pair)), (VMEM,) * 3,
        [VMEM, VMEM, pl.BlockSpec(memory_space=pl.ANY)] + [VMEM] * (2 * len(halos)),
        [pltpu.VMEM((depth, rows, cols), jnp.bfloat16)] * 2,
        flops=rows * 100_000, moved=rows * 40_000,
    )


def coverage(index, whole):
    total = jnp.zeros(index.shape, jnp.float32)
    for offset in range(-RADIUS, RADIUS + 1):
        inside = (index + offset >= 0) & (index + offset < whole)
        total = total + jnp.where(inside, float(RADIUS + 1 - abs(offset)), 0.0)
    return total


def tally(t):
    ones = 1.0 - t * t
    return t.reshape(-1, 8, t.shape[1]).sum(0), ones.reshape(-1, 8, t.shape[1]).sum(0)


def band(rows):
    tall = rows + 2 * REACH
    column = lax.broadcasted_iota(jnp.int32, (rows, 2 * tall), 1)
    column = jnp.where(column >= tall, column - tall, column)
    away = jnp.abs(column - REACH - lax.broadcasted_iota(jnp.int32, (rows, 2 * tall), 0))
    return jnp.maximum(RADIUS + 1 - away, 0).astype(jnp.float32).astype(jnp.bfloat16)


def filter_y(pieces, start, kind, rz, scale, beta, field):
    depth, rows, cols = field.shape
    blocks = -(-rows // MOST)
    size = -(-rows // (8 * blocks)) * 8
    both = jnp.zeros((2, 8, cols), jnp.float32)
    for at in range(0, rows, size):
        length = min(size, rows - at)
        w = band(length)
        here = slice(start + at, start + at + length)
        for i in range(depth):
            tall = pieces(i, at, length + 2 * REACH)
            top, rest = parts(tall)
            stack = jnp.concatenate([top, rest], axis=0)
            smooth = jnp.dot(w, stack, preferred_element_type=jnp.float32)
            filtered = smooth * (scale[here, :] * rz[i])
            what = kind[i, here, :]
            value = jnp.where(what == 0, filtered, jnp.where(what == 2, FAR, -FAR))
            field[i, at : at + length, :] = value
            both += jnp.stack(tally(jnp.tanh(beta * (value - 0.5))))
    return both


def joined(*refs):
    def pieces(i, at, length):
        found, first = [], 0
        for ref, low, high in refs:
            a, b = max(at, first), min(at + length, first + high - low)
            if a < b:
                found.append(ref[i, low + a - first : low + b - first, :])
            first += high - low
        return found[0] if len(found) == 1 else jnp.concatenate(found, axis=0)

    return pieces


def sides_kernel(
    chunks, beta, _, before, a, b, after, kind, rz, scale, field_a, field_b, sums
):
    edge = chunks[0][1] - chunks[0][0]
    one = joined((before, 0, REACH), (a, edge, a.shape[1]))
    both = filter_y(one, 0, kind, rz, scale, beta[0], field_a)
    one = joined((b, 0, b.shape[1]), (a, 0, edge), (after, 0, REACH))
    start = chunks[2][0] + REACH
    sums[...] = both + filter_y(one, start, kind, rz, scale, beta[0], field_b)


def middle_kernel(
    start, beta, density, below, above, weights, a, b, kind, rz, scale, sums,
    field, message, own, high, low,
):
    filter_zx(density, start, below, above, weights, own, high, low)
    one = joined((a, a.shape[1] - 2 * REACH, a.shape[1]), (own, 0, own.shape[1]), (b, 0, 2 * REACH))
    both = filter_y(one, start - REACH, kind, rz, scale, beta[0], field)
    pack(sums[...] + both, message)


def pack(both, message):
    folded = both[:, :, 0:128] + both[:, :, 128:256] + both[:, :, 256:384]
    row = jnp.sum(folded, axis=1)
    row = row[:, 0:64] + row[:, 64:128]
    line = jnp.concatenate([row[0:1], row[1:2]], axis=1)
    message[...] = jnp.broadcast_to(line, message.shape)


def newton(cells, message, level, beta, fraction):
    line = jnp.sum(message[...], axis=0, keepdims=True)
    lane = lax.broadcasted_iota(jnp.int32, line.shape, 1)
    total = jnp.sum(jnp.where(lane < 64, line, 0.0), axis=1, keepdims=True)
    bends = jnp.sum(jnp.where(lane < 64, 0.0, line), axis=1, keepdims=True)
    volume = 0.5 * (cells + total)
    step = (volume - fraction[0] * cells) / (cells + 0.5 * beta[0] * bends)
    return level[...] + jnp.broadcast_to(step, level.shape)


def again_kernel(cells, count, message, level, beta, fraction, *refs):
    fields, (sent, moved) = refs[:count], refs[count:]
    eta = newton(cells, message, level, beta, fraction)
    moved[...] = eta
    b = beta[0]
    cols = fields[0].shape[2]
    eta = jnp.tile(eta[:1], (1, cols // 128))
    both = jnp.zeros((2, 8, cols), jnp.float32)
    for field in fields:
        for i in range(field.shape[0]):
            both += jnp.stack(tally(jnp.tanh(b * (field[i] - eta))))
    pack(both, sent)


def last_kernel(cells, count, message, level, beta, fraction, *refs):
    fields, (out, moved, held, sems) = refs[:count], refs[count:]
    eta = newton(cells, message, level, beta, fraction)
    moved[0] = eta[0, 0]
    b = beta[0]
    eta = jnp.tile(eta[:1], (1, held.shape[2] // 128))
    copies = []
    for i in range(held.shape[0]):
        first = 0
        for k, field in enumerate(fields):
            rows = pl.ds(first, field.shape[1])
            first += field.shape[1]
            held[i, rows, :] = 0.5 * (1.0 + jnp.tanh(b * (field[i] - eta)))
            at = (i, rows, slice(None))
            copies.append(pltpu.make_async_copy(held.at[at], out.at[at], sems.at[i * count + k]))
            copies[-1].start()
    for copy in copies:
        copy.wait()


def local(slabs, pencils, density, cell_kind, beta, fraction):
    depth, rows, cols = density.shape
    members = slabs * pencils
    cells = float(depth * slabs * rows * pencils * cols)
    up = [(i, i + 1) for i in range(slabs - 1)]
    down = [(j, i) for i, j in up]
    side = [(i, i + 1) for i in range(pencils - 1)]
    f32 = jnp.float32

    halos = []
    source = density
    for n, (start, end) in enumerate(CHUNKS):
        last, leading = source[depth - RADIUS :, start:end], source[:RADIUS, start:end]
        below = lax.ppermute(last, "slab", up)
        above = lax.ppermute(leading, "slab", down)
        halos.append((below, above))
        if n == 0:
            source = lax.optimization_barrier(density)

    near = lax.broadcasted_iota(jnp.int32, (cols, cols), 0)
    near = jnp.abs(near - lax.broadcasted_iota(jnp.int32, (cols, cols), 1))
    wx = jnp.maximum(RADIUS + 1 - near, 0).astype(jnp.bfloat16)
    rz = 1.0 / coverage(lax.axis_index("slab") * depth + jnp.arange(depth), depth * slabs)
    cy = coverage(lax.axis_index("pencil") * rows + jnp.arange(rows), rows * pencils)
    scale = 1.0 / (cy[:, None] * coverage(jnp.arange(cols), cols)[None, :])

    smooth_a, tail, head = zx(CHUNKS[:2], density, halos[:2], wx, beta)
    smooth_b, _, _ = zx(CHUNKS[2:3], density, halos[2:3], wx, head)
    before = lax.ppermute(tail, "pencil", side)
    after = lax.ppermute(head, "pencil", [(j, i) for i, j in side])
    field = lambda n: jax.ShapeDtypeStruct((depth, n, cols), f32)
    sums = jax.ShapeDtypeStruct((2, 8, cols), f32)
    sent = jax.ShapeDtypeStruct((members, 128), f32)
    one = jax.ShapeDtypeStruct((1,), f32)
    mid, end = CHUNKS[3]
    field_a, field_b, sums = call(
        functools.partial(sides_kernel, CHUNKS),
        (field(mid - REACH), field(rows - end - REACH), sums),
        (beta, fraction, before, smooth_a, smooth_b, after, cell_kind, rz, scale),
        (VMEM,) * 3, [SMEM, SMEM, *[VMEM] * 5, SMEM, VMEM],
        flops=20_000_000, moved=10_000_000,
    )
    field_c, message = call(
        functools.partial(middle_kernel, mid), (field(end - mid + 2 * REACH), sent),
        (beta, density, *halos[3], wx, smooth_a, smooth_b, cell_kind, rz, scale, sums),
        (VMEM,) * 2, [SMEM, *[VMEM] * 7, SMEM, VMEM, VMEM],
        [pltpu.VMEM((depth, end - mid, cols), f32)]
        + [pltpu.VMEM((depth, end - mid, cols), jnp.bfloat16)] * 2,
        flops=6_000_000, moved=3_000_000,
    )
    fields = [field_a, field_c, field_b]
    count = len(fields)
    level = jnp.full((8, 128), 0.5, f32)
    scalars = [VMEM, VMEM, SMEM, SMEM]
    for step in range(ITERS):
        message = lax.all_to_all(message, DEVICES, 0, 0, tiled=True)
        ins = [message, level, beta, fraction, *fields]
        if step < ITERS - 1:
            message, level = call(
                functools.partial(again_kernel, cells, count),
                (sent, jax.ShapeDtypeStruct(level.shape, f32)), ins,
                (VMEM, VMEM), scalars + [VMEM] * count, flops=6_000_000, moved=3_600_000,
            )
    return call(
        functools.partial(last_kernel, cells, count), (field(rows), one), ins,
        (pl.BlockSpec(memory_space=pl.ANY), SMEM), scalars + [VMEM] * count,
        [pltpu.VMEM(density.shape, f32), pltpu.SemaphoreType.DMA((count * depth,))],
        flops=6_000_000, moved=7_200_000,
    )


def solution(mesh):
    P = jax.sharding.PartitionSpec
    grid = P("slab", "pencil", None)
    return jax.shard_map(
        functools.partial(local, mesh.shape["slab"], mesh.shape["pencil"]),
        mesh=mesh,
        in_specs=(grid, grid, P(), P()),
        out_specs=(grid, P()),
        check_vma=False,
    )
```

profile of v0, /device:TPU:2, one launch (start us, length us, event | category | flops | bytes accessed | tf_op | source)
XLA Modules:
  0.0 172.2 jit_solution(11670670946450475124)
XLA Ops:
  0.6 0.0 copy-start
  0.6 3.1 %fusion.85 = (f32[5,128,384]{2,1,0:T(8,128)}, f32[5,128,384]{2,1,0:T(8,128)}) fusion(f32[6,384,384]{2,1,0:T(8,128)} %density.5), kind=kLoop, calls=%fused_computation.112 | loop fusion | bytes 3932160 | tf_op jit(solution)/shard_map/slice | solution.py:232
  3.8 3.5 %collective-permute-start.4 = (f32[5,128,384]{2,1,0:T(8,128)}, f32[5,128,384]{2,1,0:T(8,128)}, u32[]{:S(2)}, u32[]{:S(2)}) collective-permute-start(f32[5,128,384]{2,1,0:T(8,128)} %get-tuple-element.31), channel_id=1, source_target_pairs={{0,2},{2,4},{4,6},{6,8},{8,10},{10,12},{12,14},{14,16},{16,18},{18... | collective-permute-start | bytes 2949128 | tf_op jit(solution)/shard_map/ppermute | solution.py:233
  7.2 0.0 copy-done
  7.3 0.9 fusion.86
  8.2 3.5 %collective-permute-start.2 = (f32[5,64,384]{2,1,0:T(8,128)S(1)}, f32[5,64,384]{2,1,0:T(8,128)S(1)}, u32[]{:S(2)}, u32[]{:S(2)}) collective-permute-start(f32[5,64,384]{2,1,0:T(8,128)S(1)} %get-tuple-element.33), channel_id=1, source_target_pairs={{0,2},{2,4},{4,6},{6,8},{8,10},{10,12},{12,14},{14,16},{16,18},{18... | collective-permute-start | bytes 1474568 | tf_op jit(solution)/shard_map/ppermute | solution.py:233
  11.6 1.5 fusion.84
  13.2 3.2 %collective-permute-start.6 = (f32[5,144,384]{2,1,0:T(8,128)}, f32[5,144,384]{2,1,0:T(8,128)}, u32[]{:S(2)}, u32[]{:S(2)}) collective-permute-start(f32[5,144,384]{2,1,0:T(8,128)} %get-tuple-element.29), channel_id=1, source_target_pairs={{0,2},{2,4},{4,6},{6,8},{8,10},{10,12},{12,14},{14,16},{16,18},{18... | collective-permute-start | bytes 3317768 | tf_op jit(solution)/shard_map/ppermute | solution.py:233
  16.4 6.9 %collective-permute-start.7 = (f32[5,144,384]{2,1,0:T(8,128)}, f32[5,144,384]{2,1,0:T(8,128)}, u32[]{:S(2)}, u32[]{:S(2)}) collective-permute-start(f32[5,144,384]{2,1,0:T(8,128)} %get-tuple-element.28), channel_id=1, source_target_pairs={{2,0},{4,2},{6,4},{8,6},{10,8},{12,10},{14,12},{16,14},{18,16},{20... | collective-permute-start | bytes 3317768 | tf_op jit(solution)/shard_map/ppermute | solution.py:234
  23.2 2.8 %collective-permute-start.5 = (f32[5,128,384]{2,1,0:T(8,128)}, f32[5,128,384]{2,1,0:T(8,128)}, u32[]{:S(2)}, u32[]{:S(2)}) collective-permute-start(f32[5,128,384]{2,1,0:T(8,128)} %get-tuple-element.30), channel_id=1, source_target_pairs={{2,0},{4,2},{6,4},{8,6},{10,8},{12,10},{14,12},{16,14},{18,16},{20... | collective-permute-start | bytes 2949128 | tf_op jit(solution)/shard_map/ppermute | solution.py:234
  26.1 21.2 %collective-permute-done.2.refs_0_ = f32[5,64,384]{2,1,0:T(8,128)S(1)} collective-permute-done((f32[5,64,384]{2,1,0:T(8,128)S(1)}, f32[5,64,384]{2,1,0:T(8,128)S(1)}, u32[]{:S(2)}, u32[]{:S(2)}) %collective-permute-start.2) | collective-permute-done | bytes 491552 | tf_op jit(solution)/shard_map/ppermute | solution.py:233
  47.3 0.0 copy-start.4
  47.3 0.8 copy-done.4
  48.1 3.9 %collective-permute-start.3 = (f32[5,64,384]{2,1,0:T(8,128)}, f32[5,64,384]{2,1,0:T(8,128)}, u32[]{:S(2)}, u32[]{:S(2)}) collective-permute-start(f32[5,64,384]{2,1,0:T(8,128)} %get-tuple-element.32), channel_id=1, source_target_pairs={{2,0},{4,2},{6,4},{8,6},{10,8},{12,10},{14,12},{16,14},{18,16},{20... | collective-permute-start | bytes 1474568 | tf_op jit(solution)/shard_map/ppermute | solution.py:234
  52.0 0.8 maximum_convert_fusion.weights
  52.9 0.9 fusion.87
  53.8 24.1 %collective-permute-done.3.refs_1_ = f32[5,64,384]{2,1,0:T(8,128)} collective-permute-done((f32[5,64,384]{2,1,0:T(8,128)}, f32[5,64,384]{2,1,0:T(8,128)}, u32[]{:S(2)}, u32[]{:S(2)}) %collective-permute-start.3) | collective-permute-done | bytes 491552 | tf_op jit(solution)/shard_map/ppermute | solution.py:234
  77.9 1.9 %collective-permute-start = (f32[5,48,384]{2,1,0:T(8,128)}, f32[5,48,384]{2,1,0:T(8,128)}, u32[]{:S(2)}, u32[]{:S(2)}) collective-permute-start(f32[5,48,384]{2,1,0:T(8,128)} %get-tuple-element.35), channel_id=1, source_target_pairs={{0,2},{2,4},{4,6},{6,8},{8,10},{10,12},{12,14},{14,16},{16,18},{18... | collective-permute-start | bytes 1105928 | tf_op jit(solution)/shard_map/ppermute | solution.py:233
  79.8 0.0 collective-permute-done.4.refs_2_
  79.9 8.6 %collective-permute-start.1 = (f32[5,48,384]{2,1,0:T(8,128)}, f32[5,48,384]{2,1,0:T(8,128)}, u32[]{:S(2)}, u32[]{:S(2)}) collective-permute-start(f32[5,48,384]{2,1,0:T(8,128)} %get-tuple-element.34), channel_id=1, source_target_pairs={{2,0},{4,2},{6,4},{8,6},{10,8},{12,10},{14,12},{16,14},{18,16},{20... | collective-permute-start | bytes 1105928 | tf_op jit(solution)/shard_map/ppermute | solution.py:234
  89.8 0.1 multiply_divide_fusion.scale
  90.0 0.0 collective-permute-done.5.refs_3_
  90.0 0.0 copy-start.2
  90.0 1.0 copy-done.2
  90.9 0.0 copy-start.5
  90.9 1.0 copy-done.5
  92.0 0.0 copy-start.3
  92.0 3.8 %shard_map.59 = (f32[6,192,384]{2,1,0:T(8,128)S(1)}, f32[6,8,384]{2,1,0:T(8,128)S(1)}, f32[6,8,384]{2,1,0:T(8,128)S(1)}) custom-call(f32[6,384,384]{2,1,0:T(8,128)S(1)} %copy-done, bf16[384,384]{1,0:T(8,128)(2,1)S(1)} %copy-done.2, f32[1]{0:T(128)S(6)} %copy.9._.beta, f32[5,64,384]{2,1,0:T(8,128)S(1)} %copy-done.5, ...), custom_call_target="tpu_custom_call" | custom-call | flops 19200000 | bytes 7680000 | tf_op jit(solution)/shard_map/pallas_call | solution.py:25
  95.7 1.3 collective-permute-start.9
  97.0 0.0 collective-permute-done.6.refs_0_
  97.1 3.0 %collective-permute-start.8 = (f32[6,8,384]{2,1,0:T(8,128)S(1)}, f32[6,8,384]{2,1,0:T(8,128)S(1)}, u32[]{:S(2)}, u32[]{:S(2)}) collective-permute-start(f32[6,8,384]{2,1,0:T(8,128)S(1)} %get-tuple-element.18), channel_id=1, source_target_pairs={{0,1},{2,3},{4,5},{6,7},{8,9},{10,11},{12,13},{14,15},{16,17},{18,... | collective-permute-start | bytes 221192 | tf_op jit(solution)/shard_map/ppermute | solution.py:248
  100.1 0.0 copy-start.1
  100.1 0.0 collective-permute-done.7.refs_1_
  100.1 0.0 copy-done.3
  100.2 3.8 %shard_map.60 = (f32[6,144,384]{2,1,0:T(8,128)S(1)}, f32[6,8,384]{2,1,0:T(8,128)}, f32[6,8,384]{2,1,0:T(8,128)}) custom-call(f32[6,384,384]{2,1,0:T(8,128)S(1)} %copy-done, bf16[384,384]{1,0:T(8,128)(2,1)S(1)} %copy-done.3, f32[6,8,384]{2,1,0:T(8,128)S(1)} %get-tuple-element.16._, f32[5,144,384]{2,1,0:T(8,128)} %collective-permute-done.6.refs_0_, ...), custom_call_target="tpu_custom_call" | custom-call | flops 14400000 | bytes 5760000 | tf_op jit(solution)/shard_map/pallas_call | solution.py:25
  103.9 0.0 collective-permute-done.9.after
  103.9 0.0 collective-permute-done.8.before
  104.0 0.0 copy-done.1
  104.0 2.6 %shard_map.61 = (f32[6,120,384]{2,1,0:T(8,128)S(1)}, f32[6,200,384]{2,1,0:T(8,128)S(1)}, f32[2,8,384]{2,1,0:T(8,128)S(1)}) custom-call(f32[1]{0:T(128)S(6)} %copy.9._.beta, f32[1]{0:T(128)S(6)} %copy.10._.fraction, f32[6,8,384]{2,1,0:T(8,128)S(1)} %collective-permute-done.8.before, f32[6,192,384]{2,1,0:T(8,128)S(1)} %get-tuple-element.15.a, ...), custom_call_target="tpu_custom_call" | custom-call | flops 20000000 | bytes 10000000 | tf_op jit(solution)/shard_map/pallas_call | solution.py:25
  106.6 0.0 collective-permute-done.below
  106.6 0.0 collective-permute-done.1.above
  106.6 2.2 %shard_map.62 = (f32[6,64,384]{2,1,0:T(8,128)S(1)}, f32[256,128]{1,0:T(8,128)S(1)}) custom-call(f32[1]{0:T(128)S(6)} %copy.9._.beta, f32[6,384,384]{2,1,0:T(8,128)S(1)} %copy-done, f32[5,48,384]{2,1,0:T(8,128)} %collective-permute-done.below, f32[5,48,384]{2,1,0:T(8,128)} %collective-permute-done.1.above, bf16[384,384]{1,0:T(8,128)(2,1)S(1)} %copy-done.3, ...), custom_call_target="tpu_custom_call" | custom-call | flops 6000000 | bytes 3000000 | tf_op jit(solution)/shard_map/pallas_call | solution.py:25
  108.9 21.9 %all_to_all.33 = f32[256,1,128]{2,1,0:T(1,128)S(1)} all-to-all(f32[256,1,128]{2,1,0:T(1,128)S(1)} %bitcast.15), channel_id=1, replica_groups=mesh['slab'=128,'pencil'=2] {'slab','pencil'}, dimensions={0} | all-to-all | bytes 262144 | tf_op jit(solution)/shard_map/all_to_all | solution.py:275
  130.8 1.1 shard_map.63
  131.9 18.2 %all_to_all.34 = f32[256,1,128]{2,1,0:T(1,128)S(1)} all-to-all(f32[256,1,128]{2,1,0:T(1,128)S(1)} %bitcast.16), channel_id=1, replica_groups=mesh['slab'=128,'pencil'=2] {'slab','pencil'}, dimensions={0} | all-to-all | bytes 262144 | tf_op jit(solution)/shard_map/all_to_all | solution.py:275
  150.1 1.1 shard_map.64
  151.2 18.2 %all_to_all.35 = f32[256,1,128]{2,1,0:T(1,128)S(1)} all-to-all(f32[256,1,128]{2,1,0:T(1,128)S(1)} %bitcast.17), channel_id=1, replica_groups=mesh['slab'=128,'pencil'=2] {'slab','pencil'}, dimensions={0} | all-to-all | bytes 262144 | tf_op jit(solution)/shard_map/all_to_all | solution.py:275
  169.4 2.6 %shard_map.65 = (f32[6,384,384]{2,1,0:T(8,128)}, f32[1]{0:T(128)}) custom-call(f32[256,128]{1,0:T(8,128)S(1)} %bitcast.12, f32[8,128]{1,0:T(8,128)S(1)} %get-tuple-element.27.level, f32[1]{0:T(128)S(6)} %copy.9._.beta, f32[1]{0:T(128)S(6)} %copy.10._.fraction, f32[6,120,384]{2,1,0:T(8,128)S(1)} %get-tuple-element.21.refs_0_, ...), custom_call_target="tpu_custom_call" | custom-call | flops 6000000 | bytes 7200000 | tf_op jit(solution)/shard_map/pallas_call | solution.py:25
  (3 shorter events, 0.0 us)
Async XLA Ops:
  0.6 6.6 %copy-start = (f32[6,384,384]{2,1,0:T(8,128)S(1)}, f32[6,384,384]{2,1,0:T(8,128)}, u32[]{:S(2)}) copy-start(f32[6,384,384]{2,1,0:T(8,128)} %density.5) | copy-start | bytes 10616836
  3.8 76.1 %collective-permute-start.4 = (f32[5,128,384]{2,1,0:T(8,128)}, f32[5,128,384]{2,1,0:T(8,128)}, u32[]{:S(2)}, u32[]{:S(2)}) collective-permute-start(f32[5,128,384]{2,1,0:T(8,128)} %get-tuple-element.31), channel_id=1, source_target_pairs={{0,2},{2,4},{4,6},{6,8},{8,10},{10,12},{12,14},{14,16},{16,18},{18... | collective-permute-start | bytes 2949128 | tf_op jit(solution)/shard_map/ppermute | solution.py:233
  8.2 39.1 %collective-permute-start.2 = (f32[5,64,384]{2,1,0:T(8,128)S(1)}, f32[5,64,384]{2,1,0:T(8,128)S(1)}, u32[]{:S(2)}, u32[]{:S(2)}) collective-permute-start(f32[5,64,384]{2,1,0:T(8,128)S(1)} %get-tuple-element.33), channel_id=1, source_target_pairs={{0,2},{2,4},{4,6},{6,8},{8,10},{10,12},{12,14},{14,16},{16,18},{18... | collective-permute-start | bytes 1474568 | tf_op jit(solution)/shard_map/ppermute | solution.py:233
  13.2 83.9 %collective-permute-start.6 = (f32[5,144,384]{2,1,0:T(8,128)}, f32[5,144,384]{2,1,0:T(8,128)}, u32[]{:S(2)}, u32[]{:S(2)}) collective-permute-start(f32[5,144,384]{2,1,0:T(8,128)} %get-tuple-element.29), channel_id=1, source_target_pairs={{0,2},{2,4},{4,6},{6,8},{8,10},{10,12},{12,14},{14,16},{16,18},{18... | collective-permute-start | bytes 3317768 | tf_op jit(solution)/shard_map/ppermute | solution.py:233
  16.4 83.8 %collective-permute-start.7 = (f32[5,144,384]{2,1,0:T(8,128)}, f32[5,144,384]{2,1,0:T(8,128)}, u32[]{:S(2)}, u32[]{:S(2)}) collective-permute-start(f32[5,144,384]{2,1,0:T(8,128)} %get-tuple-element.28), channel_id=1, source_target_pairs={{2,0},{4,2},{6,4},{8,6},{10,8},{12,10},{14,12},{16,14},{18,16},{20... | collective-permute-start | bytes 3317768 | tf_op jit(solution)/shard_map/ppermute | solution.py:234
  23.2 66.7 %collective-permute-start.5 = (f32[5,128,384]{2,1,0:T(8,128)}, f32[5,128,384]{2,1,0:T(8,128)}, u32[]{:S(2)}, u32[]{:S(2)}) collective-permute-start(f32[5,128,384]{2,1,0:T(8,128)} %get-tuple-element.30), channel_id=1, source_target_pairs={{2,0},{4,2},{6,4},{8,6},{10,8},{12,10},{14,12},{16,14},{18,16},{20... | collective-permute-start | bytes 2949128 | tf_op jit(solution)/shard_map/ppermute | solution.py:234
  47.3 0.8 copy-start.4
  48.1 29.8 %collective-permute-start.3 = (f32[5,64,384]{2,1,0:T(8,128)}, f32[5,64,384]{2,1,0:T(8,128)}, u32[]{:S(2)}, u32[]{:S(2)}) collective-permute-start(f32[5,64,384]{2,1,0:T(8,128)} %get-tuple-element.32), channel_id=1, source_target_pairs={{2,0},{4,2},{6,4},{8,6},{10,8},{12,10},{14,12},{16,14},{18,16},{20... | collective-permute-start | bytes 1474568 | tf_op jit(solution)/shard_map/ppermute | solution.py:234
  77.9 28.7 %collective-permute-start = (f32[5,48,384]{2,1,0:T(8,128)}, f32[5,48,384]{2,1,0:T(8,128)}, u32[]{:S(2)}, u32[]{:S(2)}) collective-permute-start(f32[5,48,384]{2,1,0:T(8,128)} %get-tuple-element.35), channel_id=1, source_target_pairs={{0,2},{2,4},{4,6},{6,8},{8,10},{10,12},{12,14},{14,16},{16,18},{18... | collective-permute-start | bytes 1105928 | tf_op jit(solution)/shard_map/ppermute | solution.py:233
  79.9 26.8 %collective-permute-start.1 = (f32[5,48,384]{2,1,0:T(8,128)}, f32[5,48,384]{2,1,0:T(8,128)}, u32[]{:S(2)}, u32[]{:S(2)}) collective-permute-start(f32[5,48,384]{2,1,0:T(8,128)} %get-tuple-element.34), channel_id=1, source_target_pairs={{2,0},{4,2},{6,4},{8,6},{10,8},{12,10},{14,12},{16,14},{18,16},{20... | collective-permute-start | bytes 1105928 | tf_op jit(solution)/shard_map/ppermute | solution.py:234
  90.0 1.0 copy-start.2
  90.9 1.0 copy-start.5
  92.0 8.2 %copy-start.3 = (bf16[384,384]{1,0:T(8,128)(2,1)S(1)}, bf16[384,384]{1,0:T(8,128)(2,1)}, u32[]{:S(2)}) copy-start(bf16[384,384]{1,0:T(8,128)(2,1)} %maximum_convert_fusion.weights) | copy-start | bytes 884740
  95.7 8.2 %collective-permute-start.9 = (f32[6,8,384]{2,1,0:T(8,128)S(1)}, f32[6,8,384]{2,1,0:T(8,128)S(1)}, u32[]{:S(2)}, u32[]{:S(2)}) collective-permute-start(f32[6,8,384]{2,1,0:T(8,128)S(1)} %get-tuple-element.16._), channel_id=1, source_target_pairs={{1,0},{3,2},{5,4},{7,6},{9,8},{11,10},{13,12},{15,14},{17,16},{19,... | collective-permute-start | bytes 221192 | tf_op jit(solution)/shard_map/ppermute | solution.py:249
  97.1 6.9 %collective-permute-start.8 = (f32[6,8,384]{2,1,0:T(8,128)S(1)}, f32[6,8,384]{2,1,0:T(8,128)S(1)}, u32[]{:S(2)}, u32[]{:S(2)}) collective-permute-start(f32[6,8,384]{2,1,0:T(8,128)S(1)} %get-tuple-element.18), channel_id=1, source_target_pairs={{0,1},{2,3},{4,5},{6,7},{8,9},{10,11},{12,13},{14,15},{16,17},{18,... | collective-permute-start | bytes 221192 | tf_op jit(solution)/shard_map/ppermute | solution.py:248
  100.1 3.8 %copy-start.1 = (s32[6,384,384]{2,1,0:T(8,128)S(1)}, s32[6,384,384]{2,1,0:T(8,128)}, u32[]{:S(2)}) copy-start(s32[6,384,384]{2,1,0:T(8,128)} %kind.3) | copy-start | bytes 10616836
where the time goes:
time: 175 us; the launch traced here: 172 us
  blocking collectives  58.3 us (33%)
  waiting for transfers between devices  45.3 us (26%)
  starting transfers between devices  38.6 us (22%)
  Pallas kernels  17.2 us (10%)
  local copies, waits for them, and re-layouts  9.31 us (5%)
  between operations  2.34 us (1%)
    all_to_all x3, blocking collectives, local(): message = lax.all_to_all(message, DEVICES, 0, 0, tiled=True)  58.3 us
    ppermute x4, waiting for transfers between devices, local(): above = lax.ppermute(leading, 'slab', down)  24.1 us
    ppermute x4, starting transfers between devices, local(): above = lax.ppermute(leading, 'slab', down)  22.2 us
    ppermute x4, waiting for transfers between devices, local(): below = lax.ppermute(last, 'slab', up)  21.2 us
    pallas_call x7, Pallas kernels, call(): pl.pallas_call(kernel, out_shape=outs, in_specs=in_specs, out_specs=out_s...  17.2 us
    ppermute x4, starting transfers between devices, local(): below = lax.ppermute(last, 'slab', up)  12 us
    slice x4, local copies, waits for them, and re-layouts, local(): source[:RADIUS, start:end]  6.49 us
  transfers between devices with their start and end apart: 10, of which 2 were waited for; matrix products, arithmetic and copies ran while one was open for 3% of the time, Pallas kernels for 6%

commit v1 on v0

--- a/solution.py
+++ b/solution.py
@@ -13,7 +13,8 @@
 MOST = 112
 FAR = 1e30
 LIMIT = 16 << 20
-CHUNKS = ((320, 384), (0, 128), (176, 320), (128, 176))
+CHUNKS = ((288, 384), (0, 112), (144, 288), (112, 144))
+PIECE = 32
 DEVICES = ("slab", "pencil")
 
 
@@ -45,47 +46,80 @@
     return high, (x - high.astype(jnp.float32)).astype(jnp.bfloat16)
 
 
-def filter_zx(density, start, below, above, weights, out, high, low):
-    depth, rows, cols = out.shape
-    for r in range(0, rows, 16):
-        for c in range(0, cols, 128):
-            at = (slice(r, r + 16), slice(c, c + 128))
-            layers = [below[(i, *at)] for i in range(RADIUS)]
-            layers += [density[i, start + r : start + r + 16, c : c + 128] for i in range(depth)]
-            layers += [above[(i, *at)] for i in range(RADIUS)]
-            for i, value in enumerate(along_z(layers, depth)):
-                high[(i, *at)], low[(i, *at)] = parts(value)
+class Halo:
+    def __init__(self, even, odd, held, sems, first, sem):
+        rows = even.shape[1]
+        self.held, self.first, self.copies = held, first, []
+        for r in range(0, rows, PIECE):
+            n = min(PIECE, rows - r)
+            pair = []
+            for k, ref in enumerate((even, odd)):
+                here = held.at[k, :, pl.ds(first + r, n), :]
+                pair.append(pltpu.make_async_copy(ref.at[:, pl.ds(r, n), :], here, sems.at[sem, k]))
+                pair[-1].start()
+            self.copies.append(pair)
+            sem += 1
+        self.sem = sem
+
+    def wait(self, r):
+        if r % PIECE == 0:
+            for copy in self.copies[r // PIECE]:
+                copy.wait()
+
+    def layer(self, k, i, r, c):
+        r += self.first
+        return self.held[k, i, r : r + 16, c : c + 128]
+
+
+def filter_zx(density, chunks, halos, parity, weights, out, high, low):
+    depth, _, cols = out.shape
+    odd = parity[0] == 1
+    first = 0
+    for (start, end), halo in zip(chunks, halos):
+        for r in range(0, end - start, 16):
+            halo.wait(r)
+            for c in range(0, cols, 128):
+                pairs = [[halo.layer(k, i, r, c) for k in (0, 1)] for i in range(RADIUS)]
+                layers = [jnp.where(odd, e, o) for e, o in pairs]
+                layers += [
+                    density[i, start + r : start + r + 16, c : c + 128] for i in range(depth)
+                ]
+                layers += [jnp.where(odd, o, e) for e, o in pairs]
+                at = (slice(first + r, first + r + 16), slice(c, c + 128))
+                for i, value in enumerate(along_z(layers, depth)):
+                    high[(i, *at)], low[(i, *at)] = parts(value)
+        first += end - start
     w = weights[...]
     for i in range(depth):
         total = jnp.dot(low[i], w, preferred_element_type=jnp.float32)
         out[i] = total + jnp.dot(high[i], w, preferred_element_type=jnp.float32)
 
 
-def zx_kernel(chunks, density, weights, _, *refs):
-    halos, (out, tail, head, high, low) = refs[: 2 * len(chunks)], refs[2 * len(chunks) :]
-    first = 0
+def scratch_zx(depth, cols, chunks):
+    rows = sum(end - start for start, end in chunks)
+    pieces = sum(-(-(end - start) // PIECE) for start, end in chunks)
+    return [
+        *[pltpu.VMEM((depth, rows, cols), jnp.bfloat16)] * 2,
+        pltpu.VMEM((2, RADIUS, rows, cols), jnp.float32),
+        pltpu.SemaphoreType.DMA((pieces, 2)),
+    ]
+
+
+def fetch(chunks, refs, held, sems):
+    halos, first, sem = [], 0, 0
     for n, (start, end) in enumerate(chunks):
-        rows = pl.ds(first, end - start)
-        first += end - start
-        own = [r.at[:, rows, :] for r in (out, high, low)]
-        filter_zx(density, start, *halos[2 * n : 2 * n + 2], weights, *own)
-    edge, turn = chunks[0][1] - chunks[0][0], first - (chunks[-1][1] - chunks[-1][0])
+        halos.append(Halo(refs[2 * n], refs[2 * n + 1], held, sems, first, sem))
+        first, sem = first + end - start, halos[-1].sem
+    return halos
+
+
+def zx_kernel(chunks, parity, density, weights, *refs):
+    refs, (out, tail, head, high, low, held, sems) = refs[:-7], refs[-7:]
+    halos = fetch(chunks, refs, held, sems)
+    filter_zx(density, chunks, halos, parity, weights, out, high, low)
+    edge = chunks[0][1] - chunks[0][0]
     tail[...] = out[:, edge - REACH : edge, :]
-    head[...] = out[:, turn : turn + REACH, :]
-
-
-def zx(chunks, density, halos, weights, earlier):
-    depth, cols = density.shape[0], density.shape[2]
-    rows = sum(end - start for start, end in chunks)
-    shape = lambda r: jax.ShapeDtypeStruct((depth, r, cols), jnp.float32)
-    return call(
-        functools.partial(zx_kernel, chunks),
-        (shape(rows), shape(REACH), shape(REACH)),
-        (density, weights, earlier, *(h for pair in halos for h in pair)), (VMEM,) * 3,
-        [VMEM, VMEM, pl.BlockSpec(memory_space=pl.ANY)] + [VMEM] * (2 * len(halos)),
-        [pltpu.VMEM((depth, rows, cols), jnp.bfloat16)] * 2,
-        flops=rows * 100_000, moved=rows * 40_000,
-    )
+    head[...] = out[:, edge : edge + REACH, :]
 
 
 def coverage(index, whole):
@@ -144,24 +178,29 @@
     return pieces
 
 
-def sides_kernel(
-    chunks, beta, _, before, a, b, after, kind, rz, scale, field_a, field_b, sums
+def left_kernel(edge, beta, _, before, a, kind, rz, scale, field, sums):
+    one = joined((before, 0, REACH), (a, edge, a.shape[1]))
+    sums[...] = filter_y(one, 0, kind, rz, scale, beta[0], field)
+
+
+def right_kernel(
+    edge, chunk, parity, beta, density, even, odd, weights, a, after, kind, rz, scale, sums,
+    own, field, more, high, low, held, sems,
 ):
-    edge = chunks[0][1] - chunks[0][0]
-    one = joined((before, 0, REACH), (a, edge, a.shape[1]))
-    both = filter_y(one, 0, kind, rz, scale, beta[0], field_a)
-    one = joined((b, 0, b.shape[1]), (a, 0, edge), (after, 0, REACH))
-    start = chunks[2][0] + REACH
-    sums[...] = both + filter_y(one, start, kind, rz, scale, beta[0], field_b)
+    halos = fetch((chunk,), (even, odd), held, sems)
+    filter_zx(density, (chunk,), halos, parity, weights, own, high, low)
+    one = joined((own, 0, own.shape[1]), (a, 0, edge), (after, 0, REACH))
+    more[...] = sums[...] + filter_y(one, chunk[0] + REACH, kind, rz, scale, beta[0], field)
 
 
 def middle_kernel(
-    start, beta, density, below, above, weights, a, b, kind, rz, scale, sums,
-    field, message, own, high, low,
+    chunk, parity, beta, density, even, odd, weights, a, b, kind, rz, scale, sums,
+    field, message, own, high, low, held, sems,
 ):
-    filter_zx(density, start, below, above, weights, own, high, low)
+    halos = fetch((chunk,), (even, odd), held, sems)
+    filter_zx(density, (chunk,), halos, parity, weights, own, high, low)
     one = joined((a, a.shape[1] - 2 * REACH, a.shape[1]), (own, 0, own.shape[1]), (b, 0, 2 * REACH))
-    both = filter_y(one, start - REACH, kind, rz, scale, beta[0], field)
+    both = filter_y(one, chunk[0] - REACH, kind, rz, scale, beta[0], field)
     pack(sums[...] + both, message)
 
 
@@ -221,20 +260,24 @@
     depth, rows, cols = density.shape
     members = slabs * pencils
     cells = float(depth * slabs * rows * pencils * cols)
-    up = [(i, i + 1) for i in range(slabs - 1)]
-    down = [(j, i) for i, j in up]
+    pairs = [
+        [(a, b) for i in range(k, slabs - 1, 2) for a, b in ((i, i + 1), (i + 1, i))]
+        for k in (0, 1)
+    ]
+    parity = lax.axis_index("slab") % 2
     side = [(i, i + 1) for i in range(pencils - 1)]
     f32 = jnp.float32
 
     halos = []
     source = density
     for n, (start, end) in enumerate(CHUNKS):
-        last, leading = source[depth - RADIUS :, start:end], source[:RADIUS, start:end]
-        below = lax.ppermute(last, "slab", up)
-        above = lax.ppermute(leading, "slab", down)
-        halos.append((below, above))
+        for k in (0, 1):
+            first = jnp.where(parity == k, depth - RADIUS, 0)
+            part = lax.dynamic_slice_in_dim(source[:, start:end], first, RADIUS, axis=0)
+            halos.append(lax.ppermute(part, "slab", pairs[k]))
         if n == 0:
             source = lax.optimization_barrier(density)
+    parity = jnp.reshape(parity, (1,)).astype(jnp.int32)
 
     near = lax.broadcasted_iota(jnp.int32, (cols, cols), 0)
     near = jnp.abs(near - lax.broadcasted_iota(jnp.int32, (cols, cols), 1))
@@ -243,28 +286,40 @@
     cy = coverage(lax.axis_index("pencil") * rows + jnp.arange(rows), rows * pencils)
     scale = 1.0 / (cy[:, None] * coverage(jnp.arange(cols), cols)[None, :])
 
-    smooth_a, tail, head = zx(CHUNKS[:2], density, halos[:2], wx, beta)
-    smooth_b, _, _ = zx(CHUNKS[2:3], density, halos[2:3], wx, head)
-    before = lax.ppermute(tail, "pencil", side)
-    after = lax.ppermute(head, "pencil", [(j, i) for i, j in side])
     field = lambda n: jax.ShapeDtypeStruct((depth, n, cols), f32)
     sums = jax.ShapeDtypeStruct((2, 8, cols), f32)
     sent = jax.ShapeDtypeStruct((members, 128), f32)
     one = jax.ShapeDtypeStruct((1,), f32)
+    anywhere = pl.BlockSpec(memory_space=pl.ANY)
+    size_a = sum(end - start for start, end in CHUNKS[:2])
+    edge = CHUNKS[0][1] - CHUNKS[0][0]
     mid, end = CHUNKS[3]
-    field_a, field_b, sums = call(
-        functools.partial(sides_kernel, CHUNKS),
-        (field(mid - REACH), field(rows - end - REACH), sums),
-        (beta, fraction, before, smooth_a, smooth_b, after, cell_kind, rz, scale),
-        (VMEM,) * 3, [SMEM, SMEM, *[VMEM] * 5, SMEM, VMEM],
-        flops=20_000_000, moved=10_000_000,
+    smooth_a, tail, head = call(
+        functools.partial(zx_kernel, CHUNKS[:2]), (field(size_a), field(REACH), field(REACH)),
+        (parity, density, wx, *halos[:4]), (VMEM,) * 3, [SMEM, VMEM, VMEM, *[anywhere] * 4],
+        scratch_zx(depth, cols, CHUNKS[:2]), flops=20_000_000, moved=8_000_000,
+    )
+    before = lax.ppermute(tail, "pencil", side)
+    after = lax.ppermute(head, "pencil", [(j, i) for i, j in side])
+    field_a, sums_a = call(
+        functools.partial(left_kernel, edge), (field(mid - REACH), sums),
+        (beta, fraction, before, smooth_a, cell_kind, rz, scale),
+        (VMEM,) * 2, [SMEM, SMEM, *[VMEM] * 3, SMEM, VMEM], flops=10_000_000, moved=4_000_000,
+    )
+    smooth_b, field_b, sums_b = call(
+        functools.partial(right_kernel, edge, CHUNKS[2]),
+        (field(CHUNKS[2][1] - end), field(rows - end - REACH), sums),
+        (parity, beta, density, *halos[4:6], wx, smooth_a, after, cell_kind, rz, scale, sums_a),
+        (VMEM,) * 3,
+        [SMEM, SMEM, VMEM, anywhere, anywhere, *[VMEM] * 4, SMEM, VMEM, VMEM],
+        scratch_zx(depth, cols, CHUNKS[2:3]), flops=20_000_000, moved=8_000_000,
     )
     field_c, message = call(
-        functools.partial(middle_kernel, mid), (field(end - mid + 2 * REACH), sent),
-        (beta, density, *halos[3], wx, smooth_a, smooth_b, cell_kind, rz, scale, sums),
-        (VMEM,) * 2, [SMEM, *[VMEM] * 7, SMEM, VMEM, VMEM],
-        [pltpu.VMEM((depth, end - mid, cols), f32)]
-        + [pltpu.VMEM((depth, end - mid, cols), jnp.bfloat16)] * 2,
+        functools.partial(middle_kernel, CHUNKS[3]),
+        (field(end - mid + 2 * REACH), sent),
+        (parity, beta, density, *halos[6:], wx, smooth_a, smooth_b, cell_kind, rz, scale, sums_b),
+        (VMEM,) * 2, [SMEM, SMEM, VMEM, anywhere, anywhere, *[VMEM] * 4, SMEM, VMEM, VMEM],
+        [pltpu.VMEM((depth, end - mid, cols), f32), *scratch_zx(depth, cols, CHUNKS[3:])],
         flops=6_000_000, moved=3_000_000,
     )
     fields = [field_a, field_c, field_b]

time: 175 us -> 179 us (1.023)
  local copies, waits for them, and re-layouts: 9.31 us -> 20.4 us
  waiting for transfers between devices: 45.3 us -> 41.6 us
  blocking collectives: 58.3 us -> 56 us
  starting transfers between devices: 38.6 us -> 36.7 us
    unnamed x12 -> x36, local copies, waits for them, and re-layouts: 2.82 us -> 14.4 us
    slice x4 -> x8, local copies, waits for them, and re-layouts: 6.49 us -> 1.16 us  [local(): part = lax.dynamic_slice_in_dim(source[:, start:end], first, RADIUS, axis=0)]
    dynamic_slice x0 -> x4, local copies, waits for them, and re-layouts: none -> 4.88 us  [local(): part = lax.dynamic_slice_in_dim(source[:, start:end], first, RADIUS, axis=0)]
    ppermute x8, waiting for transfers between devices: 45.3 us -> 41.6 us  [local(): halos.append(lax.ppermute(part, 'slab', pairs[k]))]
    all_to_all x3, blocking collectives: 58.3 us -> 56 us  [local(): message = lax.all_to_all(message, DEVICES, 0, 0, tiled=True)]
where the time goes in v1:
time: 179 us; the launch traced here: 176 us
  blocking collectives  56 us (31%)
  waiting for transfers between devices  41.6 us (23%)
  starting transfers between devices  36.7 us (21%)
  local copies, waits for them, and re-layouts  20.4 us (11%)
  Pallas kernels  18.1 us (10%)
  between operations  2.39 us (1%)
    all_to_all x3, blocking collectives, local(): message = lax.all_to_all(message, DEVICES, 0, 0, tiled=True)  56 us
    ppermute x8, waiting for transfers between devices, local(): halos.append(lax.ppermute(part, 'slab', pairs[k]))  41.6 us
    ppermute x8, starting transfers between devices, local(): halos.append(lax.ppermute(part, 'slab', pairs[k]))  33.5 us
    pallas_call x7, Pallas kernels, call(): pl.pallas_call(kernel, out_shape=outs, in_specs=in_specs, out_specs=out_s...  18.1 us
    unnamed x36, local copies, waits for them, and re-layouts  14.4 us
    dynamic_slice x4, local copies, waits for them, and re-layouts, local(): part = lax.dynamic_slice_in_dim(source[:, start:end], first, RADIUS, axis=0)  4.88 us
  transfers between devices with their start and end apart: 10, of which 2 were waited for; matrix products, arithmetic and copies ran while one was open for 3% of the time, Pallas kernels for 6%

profile of v1, /device:TPU:2, one launch (start us, length us, event | category | flops | bytes accessed | tf_op | source)
XLA Modules:
  0.0 176.3 jit_solution(4805848838921638925)
XLA Ops:
  0.6 0.0 slice-start
  0.7 1.1 slice-done
  1.8 1.0 constant_dynamic-slice_fusion.4
  2.8 1.6 collective-permute-start.2
  4.4 0.0 slice-done.1
  4.4 1.4 constant_dynamic-slice_fusion.2
  5.8 1.2 collective-permute-start.4
  7.0 9.5 %collective-permute-start.5 = (f32[5,112,384]{2,1,0:T(8,128)}, f32[5,112,384]{2,1,0:T(8,128)S(1)}, u32[]{:S(2)}, u32[]{:S(2)}) collective-permute-start(f32[5,112,384]{2,1,0:T(8,128)} %get-tuple-element.32), channel_id=1, source_target_pairs={{2,4},{4,2},{6,8},{8,6},{10,12},{12,10},{14,16},{16,14},{18,20},{2... | collective-permute-start | bytes 2580488 | tf_op jit(solution)/shard_map/ppermute | solution.py:277
  16.5 0.0 slice-done.2
  16.5 0.0 slice-start.3
  16.6 1.7 constant_dynamic-slice_fusion
  18.2 0.0 collective-permute-start.6
  18.2 3.1 %collective-permute-start.7 = (f32[5,144,384]{2,1,0:T(8,128)}, f32[5,144,384]{2,1,0:T(8,128)}, u32[]{:S(2)}, u32[]{:S(2)}) collective-permute-start(f32[5,144,384]{2,1,0:T(8,128)} %get-tuple-element.30), channel_id=1, source_target_pairs={{2,4},{4,2},{6,8},{8,6},{10,12},{12,10},{14,16},{16,14},{18,20},{2... | collective-permute-start | bytes 3317768 | tf_op jit(solution)/shard_map/ppermute | solution.py:277
  21.4 0.8 collective-permute-done.2.refs_0_
  22.1 0.9 copy-done.13
  23.0 10.2 %collective-permute-start.3 = (f32[5,96,384]{2,1,0:T(8,128)}, f32[5,96,384]{2,1,0:T(8,128)S(1)}, u32[]{:S(2)}, u32[]{:S(2)}) collective-permute-start(f32[5,96,384]{2,1,0:T(8,128)} %get-tuple-element.34), channel_id=1, source_target_pairs={{2,4},{4,2},{6,8},{8,6},{10,12},{12,10},{14,16},{16,14},{18,20},{2... | collective-permute-start | bytes 2211848 | tf_op jit(solution)/shard_map/ppermute | solution.py:277
  33.2 0.0 copy-start.14
  33.2 0.1 maximum_convert_fusion.weights
  33.4 0.0 slice-done.3
  33.4 0.0 copy-start.7
  33.4 0.8 constant_dynamic-slice_fusion.6
  34.2 40.8 %collective-permute-done.3.refs_1_ = f32[5,96,384]{2,1,0:T(8,128)S(1)} collective-permute-done((f32[5,96,384]{2,1,0:T(8,128)}, f32[5,96,384]{2,1,0:T(8,128)S(1)}, u32[]{:S(2)}, u32[]{:S(2)}) %collective-permute-start.3) | collective-permute-done | bytes 737312 | tf_op jit(solution)/shard_map/ppermute | solution.py:277
  75.0 0.9 copy-done.15
  75.9 0.0 collective-permute-start
  75.9 0.0 collective-permute-done.4.refs_2_
  75.9 0.9 copy-done.9
  76.8 7.8 %collective-permute-start.1 = (f32[5,32,384]{2,1,0:T(8,128)}, f32[5,32,384]{2,1,0:T(8,128)}, u32[]{:S(2)}, u32[]{:S(2)}) collective-permute-start(f32[5,32,384]{2,1,0:T(8,128)} %get-tuple-element.36), channel_id=1, source_target_pairs={{2,4},{4,2},{6,8},{8,6},{10,12},{12,10},{14,16},{16,14},{18,20},{2... | collective-permute-start | bytes 737288 | tf_op jit(solution)/shard_map/ppermute | solution.py:277
  84.7 0.0 collective-permute-done.5.refs_3_
  84.7 0.0 copy-start.11
  84.7 0.9 copy-done.11
  85.6 0.0 copy-done.14
  85.6 2.0 %copy-done = f32[6,384,384]{2,1,0:T(8,128)S(1)} copy-done((f32[6,384,384]{2,1,0:T(8,128)S(1)}, f32[6,384,384]{2,1,0:T(8,128)}, u32[]{:S(2)}) %copy-start) | copy-done | bytes 3538968
  87.6 1.2 copy-done.10
  88.8 1.2 copy-done.12
  89.9 1.1 copy-done.16
  91.0 4.1 %shard_map.59 = (f32[6,208,384]{2,1,0:T(8,128)S(1)}, f32[6,8,384]{2,1,0:T(8,128)}, f32[6,8,384]{2,1,0:T(8,128)S(1)}) custom-call(s32[1]{0:T(128)} %bitcast.parity, f32[6,384,384]{2,1,0:T(8,128)S(1)} %copy-done, bf16[384,384]{1,0:T(8,128)(2,1)S(1)} %maximum_convert_fusion.weights, f32[5,96,384]{2,1,0:T(8,128)S(1)} %copy-done.14, ...), custom_call_target="tpu_custom_call" | custom-call | flops 20000000 | bytes 8000000 | tf_op jit(solution)/shard_map/pallas_call | solution.py:26
  95.1 0.0 copy-done.7
  95.1 0.0 copy-start.3
  95.1 1.2 copy-done.3
  96.4 0.6 copy-done.17
  97.0 1.9 %collective-permute-start.9 = (f32[6,8,384]{2,1,0:T(8,128)}, f32[6,8,384]{2,1,0:T(8,128)}, u32[]{:S(2)}, u32[]{:S(2)}) collective-permute-start(f32[6,8,384]{2,1,0:T(8,128)} %get-tuple-element.18), channel_id=1, source_target_pairs={{0,1},{2,3},{4,5},{6,7},{8,9},{10,11},{12,13},{14,15},{16,17},{18,... | collective-permute-start | bytes 221192 | tf_op jit(solution)/shard_map/ppermute | solution.py:302
  98.9 1.0 multiply_divide_fusion.scale
  101.2 0.0 collective-permute-done.9.before
  101.2 1.3 collective-permute-start.8
  102.5 0.0 copy-done.2
  102.6 0.0 copy-start.4
  102.6 1.5 copy-done.4
  104.1 1.1 copy-done.6
  105.2 1.7 shard_map.60
  106.9 0.0 collective-permute-done.8.after
  106.9 0.0 collective-permute-done.6.even
  106.9 0.0 collective-permute-done.7.odd
  106.9 0.3 copy-done.1
  107.2 0.6 copy-done.5
  107.8 4.8 %shard_map.61 = (f32[6,144,384]{2,1,0:T(8,128)S(1)}, f32[6,232,384]{2,1,0:T(8,128)S(1)}, f32[2,8,384]{2,1,0:T(8,128)S(1)}) custom-call(s32[1]{0:T(128)} %bitcast.parity, f32[1]{0:T(128)S(6)} %copy.9.beta, f32[6,384,384]{2,1,0:T(8,128)S(1)} %copy-done.1, f32[5,144,384]{2,1,0:T(8,128)} %collective-permute-done.6.even, ...), custom_call_target="tpu_custom_call" | custom-call | flops 20000000 | bytes 8000000 | tf_op jit(solution)/shard_map/pallas_call | solution.py:26
  112.6 0.0 collective-permute-done.even
  112.6 0.0 collective-permute-done.1.odd
  112.6 2.7 %shard_map.62 = (f32[6,48,384]{2,1,0:T(8,128)S(1)}, f32[256,128]{1,0:T(8,128)S(1)}) custom-call(s32[1]{0:T(128)} %bitcast.parity, f32[1]{0:T(128)S(6)} %copy.9.beta, f32[6,384,384]{2,1,0:T(8,128)S(1)} %copy-done.1, f32[5,32,384]{2,1,0:T(8,128)} %collective-permute-done.even, f32[5,32,384]{2,1,0:T(8,128)} %collective-permute-done.1.odd, ...), custom_call_target="tpu_custom_call" | custom-call | flops 6000000 | bytes 3000000 | tf_op jit(solution)/shard_map/pallas_call | solution.py:26
  115.3 19.7 %all_to_all.33 = f32[256,1,128]{2,1,0:T(1,128)S(1)} all-to-all(f32[256,1,128]{2,1,0:T(1,128)S(1)} %bitcast.16), channel_id=1, replica_groups=mesh['slab'=128,'pencil'=2] {'slab','pencil'}, dimensions={0} | all-to-all | bytes 262144 | tf_op jit(solution)/shard_map/all_to_all | solution.py:330
  134.9 1.1 shard_map.63
  136.0 18.2 %all_to_all.34 = f32[256,1,128]{2,1,0:T(1,128)S(1)} all-to-all(f32[256,1,128]{2,1,0:T(1,128)S(1)} %bitcast.17), channel_id=1, replica_groups=mesh['slab'=128,'pencil'=2] {'slab','pencil'}, dimensions={0} | all-to-all | bytes 262144 | tf_op jit(solution)/shard_map/all_to_all | solution.py:330
  154.2 1.1 shard_map.64
  155.3 18.2 %all_to_all.35 = f32[256,1,128]{2,1,0:T(1,128)S(1)} all-to-all(f32[256,1,128]{2,1,0:T(1,128)S(1)} %bitcast.18), channel_id=1, replica_groups=mesh['slab'=128,'pencil'=2] {'slab','pencil'}, dimensions={0} | all-to-all | bytes 262144 | tf_op jit(solution)/shard_map/all_to_all | solution.py:330
  173.5 2.6 %shard_map.65 = (f32[6,384,384]{2,1,0:T(8,128)}, f32[1]{0:T(128)}) custom-call(f32[256,128]{1,0:T(8,128)S(1)} %bitcast.13, f32[8,128]{1,0:T(8,128)S(1)} %get-tuple-element.29.level, f32[1]{0:T(128)S(6)} %copy.9.beta, f32[1]{0:T(128)S(6)} %copy.10._.fraction, f32[6,104,384]{2,1,0:T(8,128)S(1)} %get-tuple-element.23.refs_0_, ...), custom_call_target="tpu_custom_call" | custom-call | flops 6000000 | bytes 7200000 | tf_op jit(solution)/shard_map/pallas_call | solution.py:26
  (19 shorter events, 0.1 us)
Async XLA Ops:
  0.6 1.2 slice-start
  2.8 1.6 slice-start.1
  2.8 19.4 %collective-permute-start.2 = (f32[5,96,384]{2,1,0:T(8,128)S(1)}, f32[5,96,384]{2,1,0:T(8,128)S(1)}, u32[]{:S(2)}, u32[]{:S(2)}) collective-permute-start(f32[5,96,384]{2,1,0:T(8,128)S(1)} %get-tuple-element.35), channel_id=1, source_target_pairs={{0,2},{2,0},{4,6},{6,4},{8,10},{10,8},{12,14},{14,12},{16,18},{18,... | collective-permute-start | bytes 2211848 | tf_op jit(solution)/shard_map/ppermute | solution.py:277
  5.8 70.1 %collective-permute-start.4 = (f32[5,112,384]{2,1,0:T(8,128)}, f32[5,112,384]{2,1,0:T(8,128)S(1)}, u32[]{:S(2)}, u32[]{:S(2)}) collective-permute-start(f32[5,112,384]{2,1,0:T(8,128)} %get-tuple-element.33), channel_id=1, source_target_pairs={{0,2},{2,0},{4,6},{6,4},{8,10},{10,8},{12,14},{14,12},{16,18},{18,... | collective-permute-start | bytes 2580488 | tf_op jit(solution)/shard_map/ppermute | solution.py:277
  7.0 9.6 %slice-start.2 = ((f32[6,384,384]{2,1,0:T(8,128)}), f32[6,144,384]{2,1,0:T(8,128)S(1)}, s32[]{:S(2)}) async-start(f32[6,384,384]{2,1,0:T(8,128)} %density.5), calls=%async_computation.5 | async-start | bytes 2654208 | tf_op jit(solution)/shard_map/slice | solution.py:276
  7.0 77.7 %collective-permute-start.5 = (f32[5,112,384]{2,1,0:T(8,128)}, f32[5,112,384]{2,1,0:T(8,128)S(1)}, u32[]{:S(2)}, u32[]{:S(2)}) collective-permute-start(f32[5,112,384]{2,1,0:T(8,128)} %get-tuple-element.32), channel_id=1, source_target_pairs={{2,4},{4,2},{6,8},{8,6},{10,12},{12,10},{14,16},{16,14},{18,20},{2... | collective-permute-start | bytes 2580488 | tf_op jit(solution)/shard_map/ppermute | solution.py:277
  16.5 16.8 %slice-start.3 = ((f32[6,384,384]{2,1,0:T(8,128)}), f32[6,32,384]{2,1,0:T(8,128)S(1)}, s32[]{:S(2)}) async-start(f32[6,384,384]{2,1,0:T(8,128)} %density.5), calls=%async_computation.6 | async-start | bytes 589824 | tf_op jit(solution)/shard_map/slice | solution.py:276
  18.2 88.6 %collective-permute-start.6 = (f32[5,144,384]{2,1,0:T(8,128)}, f32[5,144,384]{2,1,0:T(8,128)}, u32[]{:S(2)}, u32[]{:S(2)}) collective-permute-start(f32[5,144,384]{2,1,0:T(8,128)} %get-tuple-element.31), channel_id=1, source_target_pairs={{0,2},{2,0},{4,6},{6,4},{8,10},{10,8},{12,14},{14,12},{16,18},{18,... | collective-permute-start | bytes 3317768 | tf_op jit(solution)/shard_map/ppermute | solution.py:277
  18.2 88.7 %collective-permute-start.7 = (f32[5,144,384]{2,1,0:T(8,128)}, f32[5,144,384]{2,1,0:T(8,128)}, u32[]{:S(2)}, u32[]{:S(2)}) collective-permute-start(f32[5,144,384]{2,1,0:T(8,128)} %get-tuple-element.30), channel_id=1, source_target_pairs={{2,4},{4,2},{6,8},{8,6},{10,12},{12,10},{14,16},{16,14},{18,20},{2... | collective-permute-start | bytes 3317768 | tf_op jit(solution)/shard_map/ppermute | solution.py:277
  22.1 0.9 copy-start.13
  23.0 52.0 %collective-permute-start.3 = (f32[5,96,384]{2,1,0:T(8,128)}, f32[5,96,384]{2,1,0:T(8,128)S(1)}, u32[]{:S(2)}, u32[]{:S(2)}) collective-permute-start(f32[5,96,384]{2,1,0:T(8,128)} %get-tuple-element.34), channel_id=1, source_target_pairs={{2,4},{4,2},{6,8},{8,6},{10,12},{12,10},{14,16},{16,14},{18,20},{2... | collective-permute-start | bytes 2211848 | tf_op jit(solution)/shard_map/ppermute | solution.py:277
  33.2 52.4 %copy-start.14 = (f32[5,96,384]{2,1,0:T(8,128)S(1)}, f32[5,96,384]{2,1,0:T(8,128)}, u32[]{:S(2)}) copy-start(f32[5,96,384]{2,1,0:T(8,128)} %copy-done.13) | copy-start | bytes 2211844
  33.4 61.7 %copy-start.7 = (bf16[384,384]{1,0:T(8,128)(2,1)}, bf16[384,384]{1,0:T(8,128)(2,1)S(1)}, u32[]{:S(2)}) copy-start(bf16[384,384]{1,0:T(8,128)(2,1)S(1)} %maximum_convert_fusion.weights) | copy-start | bytes 884740
  75.0 0.9 copy-start.15
  75.9 36.7 %collective-permute-start = (f32[5,32,384]{2,1,0:T(8,128)}, f32[5,32,384]{2,1,0:T(8,128)}, u32[]{:S(2)}, u32[]{:S(2)}) collective-permute-start(f32[5,32,384]{2,1,0:T(8,128)} %get-tuple-element.37), channel_id=1, source_target_pairs={{0,2},{2,0},{4,6},{6,4},{8,10},{10,8},{12,14},{14,12},{16,18},{18,... | collective-permute-start | bytes 737288 | tf_op jit(solution)/shard_map/ppermute | solution.py:277
  75.9 0.9 copy-start.9
  76.8 35.8 %collective-permute-start.1 = (f32[5,32,384]{2,1,0:T(8,128)}, f32[5,32,384]{2,1,0:T(8,128)}, u32[]{:S(2)}, u32[]{:S(2)}) collective-permute-start(f32[5,32,384]{2,1,0:T(8,128)} %get-tuple-element.36), channel_id=1, source_target_pairs={{2,4},{4,2},{6,8},{8,6},{10,12},{12,10},{14,16},{16,14},{18,20},{2... | collective-permute-start | bytes 737288 | tf_op jit(solution)/shard_map/ppermute | solution.py:277
  84.7 0.9 copy-start.11
  85.6 2.0 %copy-start = (f32[6,384,384]{2,1,0:T(8,128)S(1)}, f32[6,384,384]{2,1,0:T(8,128)}, u32[]{:S(2)}) copy-start(f32[6,384,384]{2,1,0:T(8,128)} %density.5) | copy-start | bytes 10616836
  87.6 1.2 copy-start.10
  88.8 1.2 copy-start.12
  89.9 1.1 copy-start.16
  91.0 11.5 %copy-start.2 = (s32[6,384,384]{2,1,0:T(8,128)S(1)}, s32[6,384,384]{2,1,0:T(8,128)}, u32[]{:S(2)}) copy-start(s32[6,384,384]{2,1,0:T(8,128)} %kind.5) | copy-start | bytes 10616836
  95.1 1.3 copy-start.3
  96.4 0.6 copy-start.17
  97.0 4.2 %collective-permute-start.9 = (f32[6,8,384]{2,1,0:T(8,128)}, f32[6,8,384]{2,1,0:T(8,128)}, u32[]{:S(2)}, u32[]{:S(2)}) collective-permute-start(f32[6,8,384]{2,1,0:T(8,128)} %get-tuple-element.18), channel_id=1, source_target_pairs={{0,1},{2,3},{4,5},{6,7},{8,9},{10,11},{12,13},{14,15},{16,17},{18,... | collective-permute-start | bytes 221192 | tf_op jit(solution)/shard_map/ppermute | solution.py:302
  101.2 5.6 %collective-permute-start.8 = (f32[6,8,384]{2,1,0:T(8,128)}, f32[6,8,384]{2,1,0:T(8,128)S(1)}, u32[]{:S(2)}, u32[]{:S(2)}) collective-permute-start(f32[6,8,384]{2,1,0:T(8,128)} %copy-done.17), channel_id=1, source_target_pairs={{1,0},{3,2},{5,4},{7,6},{9,8},{11,10},{13,12},{15,14},{17,16},{19,... | collective-permute-start | bytes 221192 | tf_op jit(solution)/shard_map/ppermute | solution.py:303
  102.6 1.5 copy-start.4
  104.1 1.1 copy-start.6
  105.1 2.0 %copy-start.1 = (f32[6,384,384]{2,1,0:T(8,128)S(1)}, f32[6,384,384]{2,1,0:T(8,128)}, u32[]{:S(2)}) copy-start(f32[6,384,384]{2,1,0:T(8,128)} %density.5) | copy-start | bytes 10616836
  105.2 2.6 %copy-start.5 = (f32[6,208,384]{2,1,0:T(8,128)S(1)}, f32[6,208,384]{2,1,0:T(8,128)}, u32[]{:S(2)}) copy-start(f32[6,208,384]{2,1,0:T(8,128)} %copy-done.3) | copy-start | bytes 5750788
  105.2 2.6 %copy-start.8 = (bf16[384,384]{1,0:T(8,128)(2,1)S(1)}, bf16[384,384]{1,0:T(8,128)(2,1)}, u32[]{:S(2)}) copy-start(bf16[384,384]{1,0:T(8,128)(2,1)} %copy-done.7) | copy-start | bytes 884740

commit v2 on v1

--- a/solution.py
+++ b/solution.py
@@ -13,7 +13,7 @@
 MOST = 112
 FAR = 1e30
 LIMIT = 16 << 20
-CHUNKS = ((288, 384), (0, 112), (144, 288), (112, 144))
+CHUNKS = ((352, 384), (0, 176), (208, 352), (176, 208))
 PIECE = 32
 DEVICES = ("slab", "pencil")
 
@@ -49,7 +49,8 @@
 class Halo:
     def __init__(self, even, odd, held, sems, first, sem):
         rows = even.shape[1]
-        self.held, self.first, self.copies = held, first, []
+        self.first, self.copies = first, []
+        self.refs = [held.at[k] for k in (0, 1)]
         for r in range(0, rows, PIECE):
             n = min(PIECE, rows - r)
             pair = []
@@ -66,40 +67,45 @@
             for copy in self.copies[r // PIECE]:
                 copy.wait()
 
-    def layer(self, k, i, r, c):
-        r += self.first
-        return self.held[k, i, r : r + 16, c : c + 128]
-
-
-def filter_zx(density, chunks, halos, parity, weights, out, high, low):
-    depth, _, cols = out.shape
-    odd = parity[0] == 1
+
+class Near:
+    def __init__(self, even, odd):
+        self.first, self.refs = 0, [even, odd]
+
+    def wait(self, r):
+        pass
+
+
+def filter_zx(density, chunks, halos, place, weights, out, halves):
+    depth, rows, cols = out.shape
+    odd, edge = place[0] == 1, place[1] == 1
     first = 0
     for (start, end), halo in zip(chunks, halos):
         for r in range(0, end - start, 16):
             halo.wait(r)
+            near = slice(halo.first + r, halo.first + r + 16)
             for c in range(0, cols, 128):
-                pairs = [[halo.layer(k, i, r, c) for k in (0, 1)] for i in range(RADIUS)]
-                layers = [jnp.where(odd, e, o) for e, o in pairs]
-                layers += [
-                    density[i, start + r : start + r + 16, c : c + 128] for i in range(depth)
-                ]
-                layers += [jnp.where(odd, o, e) for e, o in pairs]
-                at = (slice(first + r, first + r + 16), slice(c, c + 128))
+                across = slice(c, c + 128)
+                e, o = ([ref[i, near, across] for i in range(RADIUS)] for ref in halo.refs)
+                o = [jnp.where(edge, 0.0, v) for v in o]
+                layers = [jnp.where(odd, a, b) for a, b in zip(e, o)]
+                layers += [density[i, start + r : start + r + 16, across] for i in range(depth)]
+                layers += [jnp.where(odd, b, a) for a, b in zip(e, o)]
+                at = (slice(first + r, first + r + 16), across)
                 for i, value in enumerate(along_z(layers, depth)):
-                    high[(i, *at)], low[(i, *at)] = parts(value)
+                    halves[(0, i, *at)], halves[(1, i, *at)] = parts(value)
         first += end - start
-    w = weights[...]
-    for i in range(depth):
-        total = jnp.dot(low[i], w, preferred_element_type=jnp.float32)
-        out[i] = total + jnp.dot(high[i], w, preferred_element_type=jnp.float32)
+    flat = halves[...].reshape(2 * depth * rows, cols)
+    total = jnp.dot(flat, weights[...], preferred_element_type=jnp.float32)
+    total = total.reshape(2, depth, rows, cols)
+    out[...] = total[0] + total[1]
 
 
 def scratch_zx(depth, cols, chunks):
     rows = sum(end - start for start, end in chunks)
     pieces = sum(-(-(end - start) // PIECE) for start, end in chunks)
     return [
-        *[pltpu.VMEM((depth, rows, cols), jnp.bfloat16)] * 2,
+        pltpu.VMEM((2, depth, rows, cols), jnp.bfloat16),
         pltpu.VMEM((2, RADIUS, rows, cols), jnp.float32),
         pltpu.SemaphoreType.DMA((pieces, 2)),
     ]
@@ -113,10 +119,10 @@
     return halos
 
 
-def zx_kernel(chunks, parity, density, weights, *refs):
-    refs, (out, tail, head, high, low, held, sems) = refs[:-7], refs[-7:]
+def zx_kernel(chunks, place, density, weights, *refs):
+    refs, (out, tail, head, halves, held, sems) = refs[:-6], refs[-6:]
     halos = fetch(chunks, refs, held, sems)
-    filter_zx(density, chunks, halos, parity, weights, out, high, low)
+    filter_zx(density, chunks, halos, place, weights, out, halves)
     edge = chunks[0][1] - chunks[0][0]
     tail[...] = out[:, edge - REACH : edge, :]
     head[...] = out[:, edge : edge + REACH, :]
@@ -184,21 +190,20 @@
 
 
 def right_kernel(
-    edge, chunk, parity, beta, density, even, odd, weights, a, after, kind, rz, scale, sums,
-    own, field, more, high, low, held, sems,
+    edge, chunk, place, beta, density, even, odd, weights, a, after, kind, rz, scale, sums,
+    own, field, more, halves, held, sems,
 ):
     halos = fetch((chunk,), (even, odd), held, sems)
-    filter_zx(density, (chunk,), halos, parity, weights, own, high, low)
+    filter_zx(density, (chunk,), halos, place, weights, own, halves)
     one = joined((own, 0, own.shape[1]), (a, 0, edge), (after, 0, REACH))
     more[...] = sums[...] + filter_y(one, chunk[0] + REACH, kind, rz, scale, beta[0], field)
 
 
 def middle_kernel(
-    chunk, parity, beta, density, even, odd, weights, a, b, kind, rz, scale, sums,
-    field, message, own, high, low, held, sems,
+    chunk, place, beta, density, even, odd, weights, a, b, kind, rz, scale, sums,
+    field, message, own, halves,
 ):
-    halos = fetch((chunk,), (even, odd), held, sems)
-    filter_zx(density, (chunk,), halos, parity, weights, own, high, low)
+    filter_zx(density, (chunk,), (Near(even, odd),), place, weights, own, halves)
     one = joined((a, a.shape[1] - 2 * REACH, a.shape[1]), (own, 0, own.shape[1]), (b, 0, 2 * REACH))
     both = filter_y(one, chunk[0] - REACH, kind, rz, scale, beta[0], field)
     pack(sums[...] + both, message)
@@ -261,7 +266,11 @@
     members = slabs * pencils
     cells = float(depth * slabs * rows * pencils * cols)
     pairs = [
-        [(a, b) for i in range(k, slabs - 1, 2) for a, b in ((i, i + 1), (i + 1, i))]
+        [
+            (a, b)
+            for i in range(k, slabs, 2)
+            for a, b in ((i, (i + 1) % slabs), ((i + 1) % slabs, i))
+        ]
         for k in (0, 1)
     ]
     parity = lax.axis_index("slab") % 2
@@ -277,7 +286,8 @@
             halos.append(lax.ppermute(part, "slab", pairs[k]))
         if n == 0:
             source = lax.optimization_barrier(density)
-    parity = jnp.reshape(parity, (1,)).astype(jnp.int32)
+    index = lax.axis_index("slab")
+    place = jnp.stack([parity, ((index == 0) | (index == slabs - 1)).astype(jnp.int32)])
 
     near = lax.broadcasted_iota(jnp.int32, (cols, cols), 0)
     near = jnp.abs(near - lax.broadcasted_iota(jnp.int32, (cols, cols), 1))
@@ -296,7 +306,7 @@
     mid, end = CHUNKS[3]
     smooth_a, tail, head = call(
         functools.partial(zx_kernel, CHUNKS[:2]), (field(size_a), field(REACH), field(REACH)),
-        (parity, density, wx, *halos[:4]), (VMEM,) * 3, [SMEM, VMEM, VMEM, *[anywhere] * 4],
+        (place, density, wx, *halos[:4]), (VMEM,) * 3, [SMEM, VMEM, VMEM, *[anywhere] * 4],
         scratch_zx(depth, cols, CHUNKS[:2]), flops=20_000_000, moved=8_000_000,
     )
     before = lax.ppermute(tail, "pencil", side)
@@ -309,7 +319,7 @@
     smooth_b, field_b, sums_b = call(
         functools.partial(right_kernel, edge, CHUNKS[2]),
         (field(CHUNKS[2][1] - end), field(rows - end - REACH), sums),
-        (parity, beta, density, *halos[4:6], wx, smooth_a, after, cell_kind, rz, scale, sums_a),
+        (place, beta, density, *halos[4:6], wx, smooth_a, after, cell_kind, rz, scale, sums_a),
         (VMEM,) * 3,
         [SMEM, SMEM, VMEM, anywhere, anywhere, *[VMEM] * 4, SMEM, VMEM, VMEM],
         scratch_zx(depth, cols, CHUNKS[2:3]), flops=20_000_000, moved=8_000_000,
@@ -317,9 +327,9 @@
     field_c, message = call(
         functools.partial(middle_kernel, CHUNKS[3]),
         (field(end - mid + 2 * REACH), sent),
-        (parity, beta, density, *halos[6:], wx, smooth_a, smooth_b, cell_kind, rz, scale, sums_b),
-        (VMEM,) * 2, [SMEM, SMEM, VMEM, anywhere, anywhere, *[VMEM] * 4, SMEM, VMEM, VMEM],
-        [pltpu.VMEM((depth, end - mid, cols), f32), *scratch_zx(depth, cols, CHUNKS[3:])],
+        (place, beta, density, *halos[6:], wx, smooth_a, smooth_b, cell_kind, rz, scale, sums_b),
+        (VMEM,) * 2, [SMEM, SMEM, *[VMEM] * 7, SMEM, VMEM, VMEM],
+        [pltpu.VMEM((depth, end - mid, cols), f32), scratch_zx(depth, cols, CHUNKS[3:])[0]],
         flops=6_000_000, moved=3_000_000,
     )
     fields = [field_a, field_c, field_b]

time: 179 us -> 178 us (level)
  waiting for transfers between devices: 41.6 us -> 51.8 us
  starting transfers between devices: 36.7 us -> 28.8 us
  local copies, waits for them, and re-layouts: 20.4 us -> 16.2 us
    ppermute x8, waiting for transfers between devices: 41.6 us -> 51.8 us  [local(): halos.append(lax.ppermute(part, 'slab', pairs[k]))]
    ppermute x8, starting transfers between devices: 33.5 us -> 25.4 us  [local(): halos.append(lax.ppermute(part, 'slab', pairs[k]))]
    unnamed x36 -> x28, local copies, waits for them, and re-layouts: 14.4 us -> 10.3 us
  transfers between devices with their start and end apart: 10 -> 10, of which waited for: 2 -> 2; matrix products, arithmetic and copies ran while one was open for 3% -> 2% of each run, Pallas kernels for 6% -> 6%
where the time goes in v2:
time: 178 us; the launch traced here: 175 us
  blocking collectives  57 us (32%)
  waiting for transfers between devices  51.8 us (29%)
  starting transfers between devices  28.8 us (16%)
  Pallas kernels  18.1 us (10%)
  local copies, waits for them, and re-layouts  16.2 us (9%)
  between operations  2.32 us (1%)
    all_to_all x3, blocking collectives, local(): message = lax.all_to_all(message, DEVICES, 0, 0, tiled=True)  57 us
    ppermute x8, waiting for transfers between devices, local(): halos.append(lax.ppermute(part, 'slab', pairs[k]))  51.8 us
    ppermute x8, starting transfers between devices, local(): halos.append(lax.ppermute(part, 'slab', pairs[k]))  25.4 us
    pallas_call x7, Pallas kernels, call(): pl.pallas_call(kernel, out_shape=outs, in_specs=in_specs, out_specs=out_s...  18.1 us
    unnamed x28, local copies, waits for them, and re-layouts  10.3 us
    dynamic_slice x4, local copies, waits for them, and re-layouts, local(): part = lax.dynamic_slice_in_dim(source[:, start:end], first, RADIUS, axis=0)  4.42 us
  transfers between devices with their start and end apart: 10, of which 2 were waited for; matrix products, arithmetic and copies ran while one was open for 2% of the time, Pallas kernels for 6%

profile of v2, /device:TPU:2, one launch (start us, length us, event | category | flops | bytes accessed | tf_op | source)
XLA Modules:
  0.0 175.3 jit_solution(12105043647298175381)
XLA Ops:
  0.7 0.0 slice-start
  0.7 1.4 slice-done
  2.1 1.8 %constant_dynamic-slice_fusion.2 = (f32[5,176,384]{2,1,0:T(8,128)}, f32[5,176,384]{2,1,0:T(8,128)}) fusion(f32[6,176,384]{2,1,0:T(8,128)S(1)} %slice-done, s32[]{:T(128)S(6)} %select_n.219, s32[]{:T(128)S(6)} %select_n.218), kind=kLoop, calls=%fused_computation.70 | loop fusion | bytes 5406728 | tf_op jit(solution)/shard_map/dynamic_slice | solution.py:285
  3.9 0.0 slice-start.1
  3.9 1.6 collective-permute-start.4
  5.5 7.4 %collective-permute-start.5 = (f32[5,176,384]{2,1,0:T(8,128)}, f32[5,176,384]{2,1,0:T(8,128)}, u32[]{:S(2)}, u32[]{:S(2)}) collective-permute-start(f32[5,176,384]{2,1,0:T(8,128)} %get-tuple-element.30), channel_id=1, source_target_pairs={{2,4},{4,2},{6,8},{8,6},{10,12},{12,10},{14,16},{16,14},{18,20},{2... | collective-permute-start | bytes 4055048 | tf_op jit(solution)/shard_map/ppermute | solution.py:286
  12.9 0.0 slice-done.1
  12.9 0.0 slice-start.2
  12.9 1.6 constant_dynamic-slice_fusion
  14.5 0.0 slice-start.3
  14.5 0.0 collective-permute-start.6
  14.6 1.3 collective-permute-start.7
  15.9 0.0 slice-done.2
  15.9 0.8 collective-permute-start.2
  16.7 47.7 %collective-permute-done.2.refs_0_ = f32[5,32,384]{2,1,0:T(8,128)S(1)} collective-permute-done((f32[5,32,384]{2,1,0:T(8,128)S(1)}, f32[5,32,384]{2,1,0:T(8,128)S(1)}, u32[]{:S(2)}, u32[]{:S(2)}) %collective-permute-start.2) | collective-permute-done | bytes 245792 | tf_op jit(solution)/shard_map/ppermute | solution.py:286
  64.5 0.0 copy-start.11
  64.5 8.3 %collective-permute-start.3 = (f32[5,32,384]{2,1,0:T(8,128)S(1)}, f32[5,32,384]{2,1,0:T(8,128)S(1)}, u32[]{:S(2)}, u32[]{:S(2)}) collective-permute-start(f32[5,32,384]{2,1,0:T(8,128)S(1)} %get-tuple-element.34), channel_id=1, source_target_pairs={{2,4},{4,2},{6,8},{8,6},{10,12},{12,10},{14,16},{16,14},{18,20},{2... | collective-permute-start | bytes 737288 | tf_op jit(solution)/shard_map/ppermute | solution.py:286
  72.8 0.1 pad_add_fusion.place
  72.8 0.1 maximum_convert_fusion.weights
  73.0 0.0 slice-done.3
  73.0 0.0 copy-start.7
  73.0 0.9 constant_dynamic-slice_fusion.6
  73.9 4.0 %collective-permute-done.3.refs_1_ = f32[5,32,384]{2,1,0:T(8,128)S(1)} collective-permute-done((f32[5,32,384]{2,1,0:T(8,128)S(1)}, f32[5,32,384]{2,1,0:T(8,128)S(1)}, u32[]{:S(2)}, u32[]{:S(2)}) %collective-permute-start.3) | collective-permute-done | bytes 245792 | tf_op jit(solution)/shard_map/ppermute | solution.py:286
  78.0 0.0 collective-permute-start
  78.0 0.0 collective-permute-done.4.refs_2_
  78.0 0.0 copy-start.9
  78.0 1.1 copy-done.9
  79.0 6.0 %collective-permute-start.1 = (f32[5,32,384]{2,1,0:T(8,128)}, f32[5,32,384]{2,1,0:T(8,128)}, u32[]{:S(2)}, u32[]{:S(2)}) collective-permute-start(f32[5,32,384]{2,1,0:T(8,128)} %get-tuple-element.36), channel_id=1, source_target_pairs={{2,4},{4,2},{6,8},{8,6},{10,12},{12,10},{14,16},{16,14},{18,20},{2... | collective-permute-start | bytes 737288 | tf_op jit(solution)/shard_map/ppermute | solution.py:286
  85.0 0.0 copy-done.11
  85.0 0.0 collective-permute-done.5.refs_3_
  85.0 0.0 copy-start
  85.0 2.0 %copy-done = f32[6,384,384]{2,1,0:T(8,128)S(1)} copy-done((f32[6,384,384]{2,1,0:T(8,128)S(1)}, f32[6,384,384]{2,1,0:T(8,128)}, u32[]{:S(2)}) %copy-start) | copy-done | bytes 3538968
  87.0 1.3 copy-done.10
  88.3 0.9 copy-done.12
  89.3 4.9 %shard_map.59 = (f32[6,208,384]{2,1,0:T(8,128)S(1)}, f32[6,8,384]{2,1,0:T(8,128)}, f32[6,8,384]{2,1,0:T(8,128)S(1)}) custom-call(s32[2]{0:T(128)S(1)} %pad_add_fusion.place, f32[6,384,384]{2,1,0:T(8,128)S(1)} %copy-done, bf16[384,384]{1,0:T(8,128)(2,1)S(1)} %maximum_convert_fusion.weights, f32[5,32,384]{2,1,0:T(8,128)S(1)} %copy-done.12, ...), custom_call_target="tpu_custom_call" | custom-call | flops 20000000 | bytes 8000000 | tf_op jit(solution)/shard_map/pallas_call | solution.py:26
  94.2 0.0 copy-done.7
  94.2 0.0 copy-start.3
  94.3 1.2 copy-done.3
  95.5 0.6 copy-done.13
  96.1 1.9 %collective-permute-start.9 = (f32[6,8,384]{2,1,0:T(8,128)}, f32[6,8,384]{2,1,0:T(8,128)}, u32[]{:S(2)}, u32[]{:S(2)}) collective-permute-start(f32[6,8,384]{2,1,0:T(8,128)} %get-tuple-element.18), channel_id=1, source_target_pairs={{0,1},{2,3},{4,5},{6,7},{8,9},{10,11},{12,13},{14,15},{16,17},{18,... | collective-permute-start | bytes 221192 | tf_op jit(solution)/shard_map/ppermute | solution.py:312
  98.0 1.0 multiply_divide_fusion.scale
  100.3 0.0 collective-permute-done.9.before
  100.3 1.5 collective-permute-start.8
  101.8 0.0 copy-done.2
  101.8 0.0 copy-start.4
  101.8 1.5 copy-done.4
  103.4 1.1 copy-done.6
  104.4 2.1 %shard_map.60 = (f32[6,168,384]{2,1,0:T(8,128)S(1)}, f32[2,8,384]{2,1,0:T(8,128)S(1)}) custom-call(f32[1]{0:T(128)S(6)} %copy.9.beta, f32[1]{0:T(128)S(6)} %copy.10._.fraction, f32[6,8,384]{2,1,0:T(8,128)} %collective-permute-done.9.before, f32[6,208,384]{2,1,0:T(8,128)S(1)} %copy-done.4, s32[6,384,384]{2,1,0:T(8,128)S(1)} %copy-done.2, f32[6]{0:T(128)S(1)} %fusion.83.rz, ...), custom_call_target="tpu_custom_call" | custom-call | flops 10000000 | bytes 4000000 | tf_op jit(solution)/shard_map/pallas_call | solution.py:26
  106.5 0.0 collective-permute-done.6.even
  106.5 0.0 collective-permute-done.7.odd
  106.5 0.0 collective-permute-done.8.after
  106.6 0.0 copy-done.1
  106.6 0.5 copy-done.5
  107.1 0.0 copy-done.8
  107.1 4.3 %shard_map.61 = (f32[6,144,384]{2,1,0:T(8,128)S(1)}, f32[6,168,384]{2,1,0:T(8,128)S(1)}, f32[2,8,384]{2,1,0:T(8,128)S(1)}) custom-call(s32[2]{0:T(128)S(1)} %pad_add_fusion.place, f32[1]{0:T(128)S(6)} %copy.9.beta, f32[6,384,384]{2,1,0:T(8,128)S(1)} %copy-done.1, f32[5,144,384]{2,1,0:T(8,128)} %collective-permute-done.6.even, ...), custom_call_target="tpu_custom_call" | custom-call | flops 20000000 | bytes 8000000 | tf_op jit(solution)/shard_map/pallas_call | solution.py:26
  111.4 0.0 collective-permute-done.even
  111.4 0.0 collective-permute-done.1.odd
  111.4 1.9 %shard_map.62 = (f32[6,48,384]{2,1,0:T(8,128)S(1)}, f32[256,128]{1,0:T(8,128)S(1)}) custom-call(s32[2]{0:T(128)S(1)} %pad_add_fusion.place, f32[1]{0:T(128)S(6)} %copy.9.beta, f32[6,384,384]{2,1,0:T(8,128)S(1)} %copy-done.1, f32[5,32,384]{2,1,0:T(8,128)} %collective-permute-done.even, f32[5,32,384]{2,1,0:T(8,128)} %collective-permute-done.1.odd, ...), custom_call_target="tpu_custom_call" | custom-call | flops 6000000 | bytes 3000000 | tf_op jit(solution)/shard_map/pallas_call | solution.py:26
  113.3 20.7 %all_to_all.33 = f32[256,1,128]{2,1,0:T(1,128)S(1)} all-to-all(f32[256,1,128]{2,1,0:T(1,128)S(1)} %bitcast.17), channel_id=1, replica_groups=mesh['slab'=128,'pencil'=2] {'slab','pencil'}, dimensions={0} | all-to-all | bytes 262144 | tf_op jit(solution)/shard_map/all_to_all | solution.py:340
  134.0 1.1 shard_map.63
  135.1 18.2 %all_to_all.34 = f32[256,1,128]{2,1,0:T(1,128)S(1)} all-to-all(f32[256,1,128]{2,1,0:T(1,128)S(1)} %bitcast.18), channel_id=1, replica_groups=mesh['slab'=128,'pencil'=2] {'slab','pencil'}, dimensions={0} | all-to-all | bytes 262144 | tf_op jit(solution)/shard_map/all_to_all | solution.py:340
  153.3 1.1 shard_map.64
  154.4 18.2 %all_to_all.35 = f32[256,1,128]{2,1,0:T(1,128)S(1)} all-to-all(f32[256,1,128]{2,1,0:T(1,128)S(1)} %bitcast.19), channel_id=1, replica_groups=mesh['slab'=128,'pencil'=2] {'slab','pencil'}, dimensions={0} | all-to-all | bytes 262144 | tf_op jit(solution)/shard_map/all_to_all | solution.py:340
  172.5 2.6 %shard_map.65 = (f32[6,384,384]{2,1,0:T(8,128)}, f32[1]{0:T(128)}) custom-call(f32[256,128]{1,0:T(8,128)S(1)} %bitcast.14, f32[8,128]{1,0:T(8,128)S(1)} %get-tuple-element.29.level, f32[1]{0:T(128)S(6)} %copy.9.beta, f32[1]{0:T(128)S(6)} %copy.10._.fraction, f32[6,168,384]{2,1,0:T(8,128)S(1)} %get-tuple-element.23.refs_0_, ...), custom_call_target="tpu_custom_call" | custom-call | flops 6000000 | bytes 7200000 | tf_op jit(solution)/shard_map/pallas_call | solution.py:26
  (12 shorter events, 0.1 us)
Async XLA Ops:
  0.7 1.4 slice-start
  3.9 9.0 %slice-start.1 = ((f32[6,384,384]{2,1,0:T(8,128)}), f32[6,144,384]{2,1,0:T(8,128)S(1)}, s32[]{:S(2)}) async-start(f32[6,384,384]{2,1,0:T(8,128)} %density.5), calls=%async_computation.4 | async-start | bytes 2654208 | tf_op jit(solution)/shard_map/slice | solution.py:285
  3.9 74.1 %collective-permute-start.4 = (f32[5,176,384]{2,1,0:T(8,128)}, f32[5,176,384]{2,1,0:T(8,128)S(1)}, u32[]{:S(2)}, u32[]{:S(2)}) collective-permute-start(f32[5,176,384]{2,1,0:T(8,128)} %get-tuple-element.31), channel_id=1, source_target_pairs={{0,2},{2,0},{4,6},{6,4},{8,10},{10,8},{12,14},{14,12},{16,18},{18,... | collective-permute-start | bytes 4055048 | tf_op jit(solution)/shard_map/ppermute | solution.py:286
  5.5 79.5 %collective-permute-start.5 = (f32[5,176,384]{2,1,0:T(8,128)}, f32[5,176,384]{2,1,0:T(8,128)}, u32[]{:S(2)}, u32[]{:S(2)}) collective-permute-start(f32[5,176,384]{2,1,0:T(8,128)} %get-tuple-element.30), channel_id=1, source_target_pairs={{2,4},{4,2},{6,8},{8,6},{10,12},{12,10},{14,16},{16,14},{18,20},{2... | collective-permute-start | bytes 4055048 | tf_op jit(solution)/shard_map/ppermute | solution.py:286
  12.9 2.9 %slice-start.2 = ((f32[6,384,384]{2,1,0:T(8,128)}), f32[6,32,384]{2,1,0:T(8,128)S(1)}, s32[]{:S(2)}) async-start(f32[6,384,384]{2,1,0:T(8,128)} %density.5), calls=%async_computation.5 | async-start | bytes 589824 | tf_op jit(solution)/shard_map/slice | solution.py:285
  14.5 58.4 %slice-start.3 = ((f32[6,384,384]{2,1,0:T(8,128)}), f32[6,32,384]{2,1,0:T(8,128)S(1)}, s32[]{:S(2)}) async-start(f32[6,384,384]{2,1,0:T(8,128)} %density.5), calls=%async_computation.6 | async-start | bytes 589824 | tf_op jit(solution)/shard_map/slice | solution.py:285
  14.5 92.0 %collective-permute-start.6 = (f32[5,144,384]{2,1,0:T(8,128)}, f32[5,144,384]{2,1,0:T(8,128)}, u32[]{:S(2)}, u32[]{:S(2)}) collective-permute-start(f32[5,144,384]{2,1,0:T(8,128)} %get-tuple-element.33), channel_id=1, source_target_pairs={{0,2},{2,0},{4,6},{6,4},{8,10},{10,8},{12,14},{14,12},{16,18},{18,... | collective-permute-start | bytes 3317768 | tf_op jit(solution)/shard_map/ppermute | solution.py:286
  14.6 92.0 %collective-permute-start.7 = (f32[5,144,384]{2,1,0:T(8,128)}, f32[5,144,384]{2,1,0:T(8,128)}, u32[]{:S(2)}, u32[]{:S(2)}) collective-permute-start(f32[5,144,384]{2,1,0:T(8,128)} %get-tuple-element.32), channel_id=1, source_target_pairs={{2,4},{4,2},{6,8},{8,6},{10,12},{12,10},{14,16},{16,14},{18,20},{2... | collective-permute-start | bytes 3317768 | tf_op jit(solution)/shard_map/ppermute | solution.py:286
  15.9 48.6 %collective-permute-start.2 = (f32[5,32,384]{2,1,0:T(8,128)S(1)}, f32[5,32,384]{2,1,0:T(8,128)S(1)}, u32[]{:S(2)}, u32[]{:S(2)}) collective-permute-start(f32[5,32,384]{2,1,0:T(8,128)S(1)} %get-tuple-element.35), channel_id=1, source_target_pairs={{0,2},{2,0},{4,6},{6,4},{8,10},{10,8},{12,14},{14,12},{16,18},{18,... | collective-permute-start | bytes 737288 | tf_op jit(solution)/shard_map/ppermute | solution.py:286
  64.5 20.5 %copy-start.11 = (f32[5,32,384]{2,1,0:T(8,128)}, f32[5,32,384]{2,1,0:T(8,128)S(1)}, u32[]{:S(2)}) copy-start(f32[5,32,384]{2,1,0:T(8,128)S(1)} %collective-permute-done.2.refs_0_) | copy-start | bytes 737284
  64.5 13.5 %collective-permute-start.3 = (f32[5,32,384]{2,1,0:T(8,128)S(1)}, f32[5,32,384]{2,1,0:T(8,128)S(1)}, u32[]{:S(2)}, u32[]{:S(2)}) collective-permute-start(f32[5,32,384]{2,1,0:T(8,128)S(1)} %get-tuple-element.34), channel_id=1, source_target_pairs={{2,4},{4,2},{6,8},{8,6},{10,12},{12,10},{14,16},{16,14},{18,20},{2... | collective-permute-start | bytes 737288 | tf_op jit(solution)/shard_map/ppermute | solution.py:286
  73.0 21.3 %copy-start.7 = (bf16[384,384]{1,0:T(8,128)(2,1)}, bf16[384,384]{1,0:T(8,128)(2,1)S(1)}, u32[]{:S(2)}) copy-start(bf16[384,384]{1,0:T(8,128)(2,1)S(1)} %maximum_convert_fusion.weights) | copy-start | bytes 884740
  78.0 33.4 %collective-permute-start = (f32[5,32,384]{2,1,0:T(8,128)}, f32[5,32,384]{2,1,0:T(8,128)}, u32[]{:S(2)}, u32[]{:S(2)}) collective-permute-start(f32[5,32,384]{2,1,0:T(8,128)} %get-tuple-element.37), channel_id=1, source_target_pairs={{0,2},{2,0},{4,6},{6,4},{8,10},{10,8},{12,14},{14,12},{16,18},{18,... | collective-permute-start | bytes 737288 | tf_op jit(solution)/shard_map/ppermute | solution.py:286
  78.0 1.1 copy-start.9
  79.0 32.4 %collective-permute-start.1 = (f32[5,32,384]{2,1,0:T(8,128)}, f32[5,32,384]{2,1,0:T(8,128)}, u32[]{:S(2)}, u32[]{:S(2)}) collective-permute-start(f32[5,32,384]{2,1,0:T(8,128)} %get-tuple-element.36), channel_id=1, source_target_pairs={{2,4},{4,2},{6,8},{8,6},{10,12},{12,10},{14,16},{16,14},{18,20},{2... | collective-permute-start | bytes 737288 | tf_op jit(solution)/shard_map/ppermute | solution.py:286
  85.0 2.0 %copy-start = (f32[6,384,384]{2,1,0:T(8,128)S(1)}, f32[6,384,384]{2,1,0:T(8,128)}, u32[]{:S(2)}) copy-start(f32[6,384,384]{2,1,0:T(8,128)} %density.5) | copy-start | bytes 10616836
  87.0 1.3 copy-start.10
  88.3 0.9 copy-start.12
  89.3 12.5 %copy-start.2 = (s32[6,384,384]{2,1,0:T(8,128)S(1)}, s32[6,384,384]{2,1,0:T(8,128)}, u32[]{:S(2)}) copy-start(s32[6,384,384]{2,1,0:T(8,128)} %kind.5) | copy-start | bytes 10616836
  94.2 1.3 copy-start.3
  95.5 0.6 copy-start.13
  96.1 4.2 %collective-permute-start.9 = (f32[6,8,384]{2,1,0:T(8,128)}, f32[6,8,384]{2,1,0:T(8,128)}, u32[]{:S(2)}, u32[]{:S(2)}) collective-permute-start(f32[6,8,384]{2,1,0:T(8,128)} %get-tuple-element.18), channel_id=1, source_target_pairs={{0,1},{2,3},{4,5},{6,7},{8,9},{10,11},{12,13},{14,15},{16,17},{18,... | collective-permute-start | bytes 221192 | tf_op jit(solution)/shard_map/ppermute | solution.py:312
  100.3 6.2 %collective-permute-start.8 = (f32[6,8,384]{2,1,0:T(8,128)}, f32[6,8,384]{2,1,0:T(8,128)S(1)}, u32[]{:S(2)}, u32[]{:S(2)}) collective-permute-start(f32[6,8,384]{2,1,0:T(8,128)} %copy-done.13), channel_id=1, source_target_pairs={{1,0},{3,2},{5,4},{7,6},{9,8},{11,10},{13,12},{15,14},{17,16},{19,... | collective-permute-start | bytes 221192 | tf_op jit(solution)/shard_map/ppermute | solution.py:313
  101.8 1.5 copy-start.4
  103.4 1.1 copy-start.6
  104.4 2.1 %copy-start.1 = (f32[6,384,384]{2,1,0:T(8,128)S(1)}, f32[6,384,384]{2,1,0:T(8,128)}, u32[]{:S(2)}) copy-start(f32[6,384,384]{2,1,0:T(8,128)} %density.5) | copy-start | bytes 10616836
  104.4 2.6 %copy-start.5 = (f32[6,208,384]{2,1,0:T(8,128)S(1)}, f32[6,208,384]{2,1,0:T(8,128)}, u32[]{:S(2)}) copy-start(f32[6,208,384]{2,1,0:T(8,128)} %copy-done.3) | copy-start | bytes 5750788
  104.4 2.6 %copy-start.8 = (bf16[384,384]{1,0:T(8,128)(2,1)S(1)}, bf16[384,384]{1,0:T(8,128)(2,1)}, u32[]{:S(2)}) copy-start(bf16[384,384]{1,0:T(8,128)(2,1)} %copy-done.7) | copy-start | bytes 884740
